TPU v7x, 128 devices: a whole 4x4x4 slice. The times are simulated.
128 devices in a mesh: row: 8 (over z, x_hi), col: 16 (over y, x_lo, core).
Axes of the slice: x: 4 (x_hi: 2, x_lo: 2; x = x_hi * 2 + x_lo), y: 4, z: 4, core: 2. Of those that a mesh axis runs over, the one named last changes fastest.
Arguments:
- t_amps: bfloat16 [16, 16, 128, 128], P('row', 'col'), may hold values from -6 to 6
- df_slabs: bfloat16 [1024, 128, 128], P('col'), may hold values from -0.09375 to 0.09375
- drive: bfloat16 [16, 16, 128, 128], P('row', 'col'), may hold values from -6 to 6
- hole_ints: bfloat16 [16, 16, 16, 16], replicated, may hold values from -0.375 to 0.375
- eps_occ: float32 [16], replicated, may hold values from -0.8 to -0.2
- eps_vir: float32 [128], replicated, may hold values from 0.2 to 1.2
Outputs:
- new_amps: float32 [16, 16, 128, 128], P('row', 'col')
All inputs are finite; a program needn't handle non-finite values.
Results may differ from a plain program's by a relative error of at most 0.0095.
Values may be sent and summed in bfloat16 or wider, within the bound.
No kernel may reach another device: no remote copies, remote signals or barrier semaphores. Data moves between devices by JAX's collectives and lax.ppermute only.
A program may use at most 64 MiB of HBM per device.

v0:
```python
import jax
import jax.numpy as jnp
from jax import lax
from jax.experimental import pallas as pl
from jax.experimental.pallas import tpu as pltpu
from jax.sharding import PartitionSpec as P


V = 128
BF = jnp.bfloat16
F32 = jnp.float32
VMEM = pl.BlockSpec(memory_space=pltpu.VMEM)
SMEM = pl.BlockSpec(memory_space=pltpu.SMEM)
ANY = pl.BlockSpec(memory_space=pl.ANY)
CHUNK = 8
PARTS = 4


def col_swap(x, mask):
    return lax.ppermute(x, "col", [(c, c ^ mask) for c in range(16)])


def row_swap(x, mask):
    return lax.ppermute(x, "row", [(r, r ^ mask) for r in range(8)])


def params(mib=48):
    return pltpu.CompilerParams(vmem_limit_bytes=mib * 2**20)


def cost(flops, nbytes):
    return pl.CostEstimate(flops=flops, bytes_accessed=nbytes, transcendentals=0)


def ladder(amps, slabs, starts, fetch=False, kind=F32):
    pairs = amps.shape[0]
    duos = pairs // 2
    nq = slabs.shape[0]
    half = CHUNK // 2
    steps = nq // CHUNK
    nstart = len(starts)
    part = nq // PARTS
    offsets = [at for _, at in starts]

    def kern(*refs):
        refs = list(refs)
        t_ref, src_ref = refs[:2]
        s_refs, refs = refs[2 : 2 + nstart], refs[2 + nstart :]
        o_ref = refs.pop(0)
        b_ref = refs.pop(0) if fetch else src_ref
        xa, xb, acc_ref = refs[:3]
        copies = []
        if fetch:
            sems = refs[3]
            for n in range(PARTS):
                span = pl.ds(n * part, part)
                copies.append(pltpu.make_async_copy(src_ref.at[span], b_ref.at[span], sems.at[n]))
                copies[-1].start()
        for p in range(pairs):
            cols = slice((p % 2) * V, (p % 2 + 1) * V)
            if nstart:
                value = s_refs[0][offsets[0] + p]
                for ref, at in zip(s_refs[1:], offsets[1:]):
                    value = value + ref[at + p]
            else:
                value = jnp.zeros((V, V), F32)
            acc_ref[p // 2, :, cols] = value

        def first(k, q, x_ref):
            two = b_ref[pl.ds(k * CHUNK + 2 * q, 2)].reshape(2 * V, V)
            x = lax.dot_general(
                t_ref[...].reshape(pairs * V, V),
                two,
                (((1,), (1,)), ((), ())),
                preferred_element_type=F32,
            ).astype(BF)
            for p in range(pairs):
                xp = x[p * V : (p + 1) * V]
                g, h = p // 2, p % 2
                x_ref[g, 2 * q * V : (2 * q + 1) * V, h * V : (h + 1) * V] = xp[:, :V]
                x_ref[g, (2 * q + 1) * V : (2 * q + 2) * V, h * V : (h + 1) * V] = xp[:, V:]

        def second(k, g, x_ref):
            wide = jnp.concatenate([b_ref[k * CHUNK + q] for q in range(CHUNK)], axis=1)
            acc_ref[g] += jnp.dot(wide, x_ref[g], preferred_element_type=F32)

        def both(k1, x1, k2, x2):
            n = max(half, duos)
            for i in range(n):
                for q in range(i * half // n, (i + 1) * half // n):
                    first(k1, q, x1)
                for g in range(i * duos // n, (i + 1) * duos // n):
                    second(k2, g, x2)

        if fetch:
            copies[0].wait()
        for q in range(half):
            first(0, q, xa)
        if fetch:
            for copy in copies[1:]:
                copy.wait()

        def step(m, carry):
            both(2 * m + 1, xb, 2 * m, xa)
            both(2 * m + 2, xa, 2 * m + 1, xb)
            return carry

        lax.fori_loop(0, (steps - 2) // 2, step, 0)
        both(steps - 1, xb, steps - 2, xa)
        for g in range(duos):
            second(steps - 1, g, xb)
        for p in range(pairs):
            o_ref[p] = acc_ref[p // 2, :, (p % 2) * V : (p % 2 + 1) * V].astype(kind)

    shapes = [jax.ShapeDtypeStruct((pairs, V, V), kind)]
    scratch = [pltpu.VMEM((duos, CHUNK * V, 2 * V), BF)] * 2 + [pltpu.VMEM((duos, V, 2 * V), F32)]
    if fetch:
        shapes.append(jax.ShapeDtypeStruct(slabs.shape, BF))
        scratch.append(pltpu.SemaphoreType.DMA((PARTS,)))
    out = pl.pallas_call(
        kern,
        in_specs=[VMEM, ANY if fetch else VMEM] + [VMEM] * nstart,
        out_specs=[VMEM] * len(shapes),
        out_shape=shapes,
        scratch_shapes=scratch,
        compiler_params=params(),
        cost_estimate=cost(4 * pairs * nq * V**3, slabs.size * 2),
    )(amps, slabs, *[s for s, _ in starts])
    return out if fetch else out[0]


def spread_ints(ints, where):
    def kern(w_ref, h_ref, o_ref):
        r, c = w_ref[0], w_ref[1]
        line = lax.broadcasted_iota(jnp.int32, (256, 32), 0) >> 4
        pair = lax.broadcasted_iota(jnp.int32, (256, 32), 1)
        g, ii = line >> 1, line & 1
        slot = ((g & 1) << 2) | (g & 2) | (g >> 2)
        rows = jnp.where(pair == (ii << 4) + (c ^ (slot << 1)), 1.0, 0.0).astype(BF)
        picked = jnp.dot(rows, h_ref[...], preferred_element_type=F32).astype(BF)
        true = lax.broadcasted_iota(jnp.int32, (256, 512), 0)
        here = lax.broadcasted_iota(jnp.int32, (256, 512), 1)
        par, d, kk = here >> 8, (here >> 5) & 7, (here >> 4) & 1
        mask = (d & 1) | ((d & 2) << 1) | ((d & 4) >> 1)
        wanted = ((((r ^ mask) << 1) + kk) << 4) + (c ^ par)
        cols = jnp.where(true == wanted, 1.0, 0.0).astype(BF)
        wide = jnp.dot(picked, cols, preferred_element_type=F32)
        o_ref[...] = jnp.where((true & 15) == (here & 15), wide, 0.0).astype(BF)

    return pl.pallas_call(
        kern,
        in_specs=[SMEM, VMEM],
        out_specs=VMEM,
        out_shape=jax.ShapeDtypeStruct((256, 512), BF),
        compiler_params=params(),
        cost_estimate=cost(10**8, 10**6),
        name="spread",
    )(where, ints)


def hole_terms(wide, mine, other):
    def kern(w_ref, m_ref, p_ref, o_ref):
        for ga in range(8):
            rows = slice(ga * 16, (ga + 1) * 16)
            stack = jnp.concatenate(
                [m_ref[q, rows, :] for q in range(16)] + [p_ref[q, rows, :] for q in range(16)],
                axis=0,
            )
            terms = jnp.dot(w_ref[...], stack, preferred_element_type=F32)
            for n in range(16):
                o_ref[n, rows, :] = terms[n * 16 : (n + 1) * 16]

    return pl.pallas_call(
        kern,
        in_specs=[VMEM] * 3,
        out_specs=VMEM,
        out_shape=jax.ShapeDtypeStruct((16, V, V), F32),
        compiler_params=params(),
        cost_estimate=cost(10**9, 10**6),
        name="hole",
    )(wide, mine, other)


def body(t_amps, df_slabs, drive, hole_ints, eps_occ, eps_vir):
    r = lax.axis_index("row")
    c = lax.axis_index("col")
    where = jnp.stack([r, c]).astype(jnp.int32)
    own = t_amps.reshape(2, V, V)
    others = col_swap(df_slabs, 1)
    got_y2 = col_swap(own, 8)
    rows1 = row_swap(own, 1)
    ints = lax.dynamic_slice_in_dim(hole_ints, r * 2, 2, 0).reshape(32, 256)
    wide = spread_ints(ints, where)
    part_0, slabs = ladder(own, df_slabs, [], True)
    near = jnp.concatenate([own, got_y2])
    got_y1 = col_swap(near, 4)
    two_rows = jnp.concatenate([own, rows1])
    rows2 = row_swap(two_rows, 4)
    part_4 = ladder(got_y2, slabs, [])
    got_x = col_swap(jnp.concatenate([near, got_y1]), 2)
    four_rows = jnp.concatenate([two_rows, rows2])
    rows3 = row_swap(four_rows, 2)
    part_26 = ladder(got_y1, slabs, [])
    mine = jnp.concatenate([four_rows, rows3])
    other = col_swap(mine, 1)
    part_x = ladder(got_x, slabs, [])
    hole = hole_terms(wide, mine, other)
    send_x, fetched = ladder(got_x, others, [(part_x, 0), (hole, 8)], True, BF)
    back_x = col_swap(send_x, 2).astype(F32)
    full_26 = ladder(got_y1, fetched, [(part_26, 0), (hole, 4)])
    back_y1 = col_swap((full_26 + back_x[4:]).astype(BF), 4).astype(F32)
    start_04 = jnp.concatenate([part_0, part_4])
    full_04 = ladder(near, fetched, [(start_04, 0), (hole, 0)])
    total = full_04 + back_x[:4] + back_y1
    back_y2 = col_swap(total[2:].astype(BF), 8).astype(F32)
    total = total[:2] + back_y2
    occ_first = lax.dynamic_slice_in_dim(eps_occ, r * 2, 2, 0)
    occ_second = lax.dynamic_slice_in_dim(eps_occ, c, 1, 0)
    denom = (
        eps_vir[None, :, None]
        + eps_vir[None, None, :]
        - occ_first[:, None, None]
        - occ_second[:, None, None]
    )
    return ((drive.reshape(2, V, V).astype(F32) + total) / denom).reshape(2, 1, V, V)


def solution(mesh):
    placed = (
        P("row", "col", None, None),
        P("col", None, None),
        P("row", "col", None, None),
        P(),
        P(),
        P(),
    )

    return jax.shard_map(
        body, mesh=mesh, in_specs=placed, out_specs=P("row", "col", None, None), check_vma=False
    )
```

profile of v0, /device:TPU:1, one launch (start us, length us, event | category | flops | bytes accessed | tf_op | source)
XLA Modules:
  0.0 72.5 jit_solution(15328041307957749567)
XLA Ops:
  0.0 1.4 %collective-permute-start.3 = (bf16[64,128,128]{2,1,0:T(8,128)(2,1)}, bf16[64,128,128]{2,1,0:T(8,128)(2,1)}, u32[]{:S(2)}, u32[]{:S(2)}) collective-permute-start(bf16[64,128,128]{2,1,0:T(8,128)(2,1)} %refs_1_.1), channel_id=1, source_target_pairs={{0,1},{1,0},{2,3},{3,2},{4,5},{5,4},{6,7},{7,6},{8,9},{9,8},{10,11... | collective-permute-start | bytes 6291464 | tf_op jit(solution)/shard_map/ppermute | solution.py:20
  1.4 2.9 %collective-permute-start.4 = (bf16[2,128,128]{2,1,0:T(8,128)(2,1)}, bf16[2,128,128]{2,1,0:T(8,128)(2,1)S(1)}, u32[]{:S(2)}, u32[]{:S(2)}) collective-permute-start(bf16[2,128,128]{2,1,0:T(8,128)(2,1)} %bitcast.15), channel_id=1, source_target_pairs={{0,16},{16,0},{32,48},{48,32},{64,80},{80,64},{96,112},{112,96},{1... | collective-permute-start | bytes 196616 | tf_op jit(solution)/shard_map/ppermute | solution.py:24
  4.3 2.9 %collective-permute-start = (bf16[2,128,128]{2,1,0:T(8,128)(2,1)}, bf16[2,128,128]{2,1,0:T(8,128)(2,1)S(1)}, u32[]{:S(2)}, u32[]{:S(2)}) collective-permute-start(bf16[2,128,128]{2,1,0:T(8,128)(2,1)} %bitcast.16), channel_id=1, source_target_pairs={{0,8},{1,9},{2,10},{3,11},{4,12},{5,13},{6,14},{7,15},{8,0},{9,1},... | collective-permute-start | bytes 196616 | tf_op jit(solution)/shard_map/ppermute | solution.py:20
  7.2 1.9 %collective-permute-done.refs_0_ = bf16[2,128,128]{2,1,0:T(8,128)(2,1)S(1)} collective-permute-done((bf16[2,128,128]{2,1,0:T(8,128)(2,1)}, bf16[2,128,128]{2,1,0:T(8,128)(2,1)S(1)}, u32[]{:S(2)}, u32[]{:S(2)}) %collective-permute-start) | collective-permute-done | bytes 65568 | tf_op jit(solution)/shard_map/ppermute | solution.py:20
  9.2 1.5 %pad_maximum_fusion.4 = (bf16[4,128,128]{2,1,0:T(8,128)(2,1)}, bf16[4,128,128]{2,1,0:T(8,128)(2,1)S(1)}) fusion(bf16[2,128,128]{2,1,0:T(8,128)(2,1)} %bitcast.17, bf16[2,128,128]{2,1,0:T(8,128)(2,1)S(1)} %collective-permute-done.4, bf16[2,128,128]{2,1,0:T(8,128)(2,1)S(1)} %collective-permute-done.refs_0_), kind=kLoop, calls=%fused_computation.10 | loop fusion | flops 131072 | bytes 458752 | tf_op jit(solution)/shard_map/concatenate | solution.py:197
  10.7 3.6 %collective-permute-start.5 = (bf16[4,128,128]{2,1,0:T(8,128)(2,1)}, bf16[4,128,128]{2,1,0:T(8,128)(2,1)}, u32[]{:S(2)}, u32[]{:S(2)}) collective-permute-start(bf16[4,128,128]{2,1,0:T(8,128)(2,1)} %get-tuple-element.15), channel_id=1, source_target_pairs={{0,64},{16,80},{32,96},{48,112},{64,0},{80,16},{96,32},{112,48},{1... | collective-permute-start | bytes 393224 | tf_op jit(solution)/shard_map/ppermute | solution.py:24
  14.3 1.3 %collective-permute-start.1 = (bf16[4,128,128]{2,1,0:T(8,128)(2,1)S(1)}, bf16[4,128,128]{2,1,0:T(8,128)(2,1)S(1)}, u32[]{:S(2)}, u32[]{:S(2)}) collective-permute-start(bf16[4,128,128]{2,1,0:T(8,128)(2,1)S(1)} %get-tuple-element.16.refs_0_), channel_id=1, source_target_pairs={{0,4},{1,5},{2,6},{3,7},{4,0},{5,1},{6,2},{7,3},{8,12},{9,13},{10,... | collective-permute-start | bytes 393224 | tf_op jit(solution)/shard_map/ppermute | solution.py:20
  15.6 1.4 %collective-permute-done.5 = bf16[4,128,128]{2,1,0:T(8,128)(2,1)} collective-permute-done((bf16[4,128,128]{2,1,0:T(8,128)(2,1)}, bf16[4,128,128]{2,1,0:T(8,128)(2,1)}, u32[]{:S(2)}, u32[]{:S(2)}) %collective-permute-start.5) | collective-permute-done | bytes 131104 | tf_op jit(solution)/shard_map/ppermute | solution.py:24
  17.0 1.6 %collective-permute-done.1.refs_0_ = bf16[4,128,128]{2,1,0:T(8,128)(2,1)S(1)} collective-permute-done((bf16[4,128,128]{2,1,0:T(8,128)(2,1)S(1)}, bf16[4,128,128]{2,1,0:T(8,128)(2,1)S(1)}, u32[]{:S(2)}, u32[]{:S(2)}) %collective-permute-start.1) | collective-permute-done | bytes 131104 | tf_op jit(solution)/shard_map/ppermute | solution.py:20
  18.5 1.8 %fusion.1 = (bf16[8,128,128]{2,1,0:T(8,128)(2,1)}, bf16[8,128,128]{2,1,0:T(8,128)(2,1)}) fusion(bf16[2,128,128]{2,1,0:T(8,128)(2,1)} %bitcast.18, bf16[4,128,128]{2,1,0:T(8,128)(2,1)} %collective-permute-done.5, bf16[2,128,128]{2,1,0:T(8,128)(2,1)} %copy-done.3, bf16[4,128,128]{2,1,0:T(8,128)(2,1)S(1)} %collective-permute-done.1.refs_0_, ...), kind=kLoop, calls=%fused_computation.4 | loop fusion | flops 524288 | bytes 983040 | tf_op jit(solution)/shard_map/concatenate | solution.py:201
  21.7 1.1 %reshape.47.h_ref = bf16[32,256]{1,0:T(8,128)(2,1)S(1)} reshape(bf16[2,16,16,16]{3,2,1,0:T(8,128)(2,1)} %constant_dynamic-slice_fusion) | data formatting | bytes 32768 | tf_op jit(solution)/shard_map/reshape | solution.py:192
  23.7 2.9 %shard_map.64 = (f32[2,128,128]{2,1,0:T(8,128)S(1)}, bf16[64,128,128]{2,1,0:T(8,128)(2,1)S(1)}) custom-call(bf16[2,128,128]{2,1,0:T(8,128)(2,1)S(1)} %bitcast.19, bf16[64,128,128]{2,1,0:T(8,128)(2,1)S(1)} %copy-done.2), custom_call_target="tpu_custom_call" | custom-call | flops 1073741824 | bytes 2097152 | tf_op jit(solution)/shard_map/pallas_call | solution.py:120
  28.1 3.4 %collective-permute-start.7 = (bf16[16,128,128]{2,1,0:T(8,128)(2,1)S(1)}, bf16[16,128,128]{2,1,0:T(8,128)(2,1)S(1)}, u32[]{:S(2)}, u32[]{:S(2)}) collective-permute-start(bf16[16,128,128]{2,1,0:T(8,128)(2,1)S(1)} %pad_maximum_fusion.m_ref), channel_id=1, source_target_pairs={{0,1},{1,0},{2,3},{3,2},{4,5},{5,4},{6,7},{7,6},{8,9},{9,8},{10,11... | collective-permute-start | bytes 1572872 | tf_op jit(solution)/shard_map/ppermute | solution.py:20
  31.5 2.7 %shard_map.67 = f32[2,128,128]{2,1,0:T(8,128)S(1)} custom-call(bf16[2,128,128]{2,1,0:T(8,128)(2,1)S(1)} %collective-permute-done.refs_0_, bf16[64,128,128]{2,1,0:T(8,128)(2,1)S(1)} %get-tuple-element.9.refs_1_), custom_call_target="tpu_custom_call" | custom-call | flops 1073741824 | bytes 2097152 | tf_op jit(solution)/shard_map/pallas_call | solution.py:120
  34.2 7.4 %shard_map.65.refs_2_ = f32[8,128,128]{2,1,0:T(8,128)S(1)} custom-call(bf16[8,128,128]{2,1,0:T(8,128)(2,1)S(1)} %collective-permute-done.2.refs_0_, bf16[64,128,128]{2,1,0:T(8,128)(2,1)S(1)} %get-tuple-element.9.refs_1_), custom_call_target="tpu_custom_call" | custom-call | flops 4294967296 | bytes 2097152 | tf_op jit(solution)/shard_map/pallas_call | solution.py:120
  42.3 8.5 %shard_map.66 = (bf16[8,128,128]{2,1,0:T(8,128)(2,1)S(1)}, bf16[64,128,128]{2,1,0:T(8,128)(2,1)S(1)}) custom-call(bf16[8,128,128]{2,1,0:T(8,128)(2,1)S(1)} %collective-permute-done.2.refs_0_, bf16[64,128,128]{2,1,0:T(8,128)(2,1)} %collective-permute-done.3.refs_1_, f32[8,128,128]{2,1,0:T(8,128)S(1)} %shard_map.65.refs_2_, f32[16,128,128]{2,1,0:T(8,128)S(1)} %hole.1.refs_3_), custom_call_target="tpu_custom_call" | custom-call | flops 4294967296 | bytes 2097152 | tf_op jit(solution)/shard_map/pallas_call | solution.py:120
  50.8 1.4 %collective-permute-start.8 = (bf16[8,128,128]{2,1,0:T(8,128)(2,1)S(1)}, bf16[8,128,128]{2,1,0:T(8,128)(2,1)S(1)}, u32[]{:S(2)}, u32[]{:S(2)}) collective-permute-start(bf16[8,128,128]{2,1,0:T(8,128)(2,1)S(1)} %get-tuple-element.12), channel_id=1, source_target_pairs={{0,2},{1,3},{2,0},{3,1},{4,6},{5,7},{6,4},{7,5},{8,10},{9,11},{10,... | collective-permute-start | bytes 786440 | tf_op jit(solution)/shard_map/ppermute | solution.py:20
  52.3 4.2 %shard_map.69.refs_2_ = f32[4,128,128]{2,1,0:T(8,128)S(1)} custom-call(bf16[4,128,128]{2,1,0:T(8,128)(2,1)S(1)} %collective-permute-done.1.refs_0_, bf16[64,128,128]{2,1,0:T(8,128)(2,1)S(1)} %get-tuple-element.9.refs_1_), custom_call_target="tpu_custom_call" | custom-call | flops 2147483648 | bytes 2097152 | tf_op jit(solution)/shard_map/pallas_call | solution.py:120
  56.4 4.2 %shard_map.70 = f32[4,128,128]{2,1,0:T(8,128)S(1)} custom-call(bf16[4,128,128]{2,1,0:T(8,128)(2,1)S(1)} %collective-permute-done.1.refs_0_, bf16[64,128,128]{2,1,0:T(8,128)(2,1)S(1)} %get-tuple-element.10.refs_1_, f32[4,128,128]{2,1,0:T(8,128)S(1)} %shard_map.69.refs_2_, f32[16,128,128]{2,1,0:T(8,128)S(1)} %hole.1.refs_3_), custom_call_target="tpu_custom_call" | custom-call | flops 2147483648 | bytes 2097152 | tf_op jit(solution)/shard_map/pallas_call | solution.py:120
  60.8 1.4 %collective-permute-start.9 = (bf16[4,128,128]{2,1,0:T(8,128)(2,1)S(1)}, bf16[4,128,128]{2,1,0:T(8,128)(2,1)S(1)}, u32[]{:S(2)}, u32[]{:S(2)}) collective-permute-start(bf16[4,128,128]{2,1,0:T(8,128)(2,1)S(1)} %fusion.2), channel_id=1, source_target_pairs={{0,4},{1,5},{2,6},{3,7},{4,0},{5,1},{6,2},{7,3},{8,12},{9,13},{10,... | collective-permute-start | bytes 393224 | tf_op jit(solution)/shard_map/ppermute | solution.py:20
  62.1 4.2 %shard_map.68 = f32[4,128,128]{2,1,0:T(8,128)S(1)} custom-call(bf16[4,128,128]{2,1,0:T(8,128)(2,1)S(1)} %get-tuple-element.16.refs_0_, bf16[64,128,128]{2,1,0:T(8,128)(2,1)S(1)} %get-tuple-element.10.refs_1_, f32[4,128,128]{2,1,0:T(8,128)S(1)} %pad_maximum_fusion.3.refs_2_, f32[16,128,128]{2,1,0:T(8,128)S(1)} %hole.1.refs_3_), custom_call_target="tpu_custom_call" | custom-call | flops 2147483648 | bytes 2097152 | tf_op jit(solution)/shard_map/pallas_call | solution.py:120
  66.4 2.7 %collective-permute-start.10 = (bf16[2,128,128]{2,1,0:T(8,128)(2,1)S(1)}, bf16[2,128,128]{2,1,0:T(8,128)(2,1)S(1)}, u32[]{:S(2)}, u32[]{:S(2)}) collective-permute-start(bf16[2,128,128]{2,1,0:T(8,128)(2,1)S(1)} %slice.35), channel_id=1, source_target_pairs={{0,8},{1,9},{2,10},{3,11},{4,12},{5,13},{6,14},{7,15},{8,0},{9,1},... | collective-permute-start | bytes 196616 | tf_op jit(solution)/shard_map/ppermute | solution.py:20
  69.9 1.2 %collective-permute-done.10 = bf16[2,128,128]{2,1,0:T(8,128)(2,1)S(1)} collective-permute-done((bf16[2,128,128]{2,1,0:T(8,128)(2,1)S(1)}, bf16[2,128,128]{2,1,0:T(8,128)(2,1)S(1)}, u32[]{:S(2)}, u32[]{:S(2)}) %collective-permute-start.10) | collective-permute-done | bytes 65568 | tf_op jit(solution)/shard_map/ppermute | solution.py:20
  71.1 1.4 %fusion.6 = f32[2,1,128,128]{3,2,1,0:T(8,128)} fusion(f32[4,128,128]{2,1,0:T(8,128)S(1)} %fusion.3, bf16[2,128,128]{2,1,0:T(8,128)(2,1)S(1)} %collective-permute-done.10, bf16[2,1,128,128]{3,2,1,0:T(8,128)(2,1)S(1)} %copy-done.6, f32[]{:T(128)} %bitcast.5, f32[2]{0:T(128)S(1)} %dynamic_slice.10, f32[128,128]{1,0:T(8,128)S(1)} %broadcast_add_fusion), kind=kLoop, calls=%fused_computation.16 | loop fusion | flops 229376 | bytes 458764 | tf_op jit(solution)/shard_map/reshape | solution.py:225
  (40 shorter events, 5.5 us)
Async XLA Ops:
  0.0 21.0 %copy-start = (bf16[16,16,16,16]{3,2,1,0:T(8,128)(2,1)S(1)}, bf16[16,16,16,16]{3,2,1,0:T(8,128)(2,1)}, u32[]{:S(2)}) copy-start(bf16[16,16,16,16]{3,2,1,0:T(8,128)(2,1)} %param.9) | copy-start | bytes 393220
  0.0 23.7 %copy-start.2 = (bf16[64,128,128]{2,1,0:T(8,128)(2,1)S(1)}, bf16[64,128,128]{2,1,0:T(8,128)(2,1)}, u32[]{:S(2)}) copy-start(bf16[64,128,128]{2,1,0:T(8,128)(2,1)} %refs_1_.1) | copy-start | bytes 6291460
  0.0 23.7 %copy-start.1 = (bf16[2,1,128,128]{3,2,1,0:T(8,128)(2,1)S(1)}, bf16[2,1,128,128]{3,2,1,0:T(8,128)(2,1)}, u32[]{:S(2)}) copy-start(bf16[2,1,128,128]{3,2,1,0:T(8,128)(2,1)} %param.6) | copy-start | bytes 196612
  0.0 42.3 %collective-permute-start.3 = (bf16[64,128,128]{2,1,0:T(8,128)(2,1)}, bf16[64,128,128]{2,1,0:T(8,128)(2,1)}, u32[]{:S(2)}, u32[]{:S(2)}) collective-permute-start(bf16[64,128,128]{2,1,0:T(8,128)(2,1)} %refs_1_.1), channel_id=1, source_target_pairs={{0,1},{1,0},{2,3},{3,2},{4,5},{5,4},{6,7},{7,6},{8,9},{9,8},{10,11... | collective-permute-start | bytes 6291464 | tf_op jit(solution)/shard_map/ppermute | solution.py:20
  1.4 5.9 %collective-permute-start.4 = (bf16[2,128,128]{2,1,0:T(8,128)(2,1)}, bf16[2,128,128]{2,1,0:T(8,128)(2,1)S(1)}, u32[]{:S(2)}, u32[]{:S(2)}) collective-permute-start(bf16[2,128,128]{2,1,0:T(8,128)(2,1)} %bitcast.15), channel_id=1, source_target_pairs={{0,16},{16,0},{32,48},{48,32},{64,80},{80,64},{96,112},{112,96},{1... | collective-permute-start | bytes 196616 | tf_op jit(solution)/shard_map/ppermute | solution.py:24
  4.3 4.8 %collective-permute-start = (bf16[2,128,128]{2,1,0:T(8,128)(2,1)}, bf16[2,128,128]{2,1,0:T(8,128)(2,1)S(1)}, u32[]{:S(2)}, u32[]{:S(2)}) collective-permute-start(bf16[2,128,128]{2,1,0:T(8,128)(2,1)} %bitcast.16), channel_id=1, source_target_pairs={{0,8},{1,9},{2,10},{3,11},{4,12},{5,13},{6,14},{7,15},{8,0},{9,1},... | collective-permute-start | bytes 196616 | tf_op jit(solution)/shard_map/ppermute | solution.py:20
  7.2 7.0 %copy-start.3 = (bf16[2,128,128]{2,1,0:T(8,128)(2,1)}, bf16[2,128,128]{2,1,0:T(8,128)(2,1)S(1)}, u32[]{:S(2)}) copy-start(bf16[2,128,128]{2,1,0:T(8,128)(2,1)S(1)} %collective-permute-done.4) | copy-start | bytes 196612
  10.7 6.3 %collective-permute-start.5 = (bf16[4,128,128]{2,1,0:T(8,128)(2,1)}, bf16[4,128,128]{2,1,0:T(8,128)(2,1)}, u32[]{:S(2)}, u32[]{:S(2)}) collective-permute-start(bf16[4,128,128]{2,1,0:T(8,128)(2,1)} %get-tuple-element.15), channel_id=1, source_target_pairs={{0,64},{16,80},{32,96},{48,112},{64,0},{80,16},{96,32},{112,48},{1... | collective-permute-start | bytes 393224 | tf_op jit(solution)/shard_map/ppermute | solution.py:24
  14.3 4.2 %collective-permute-start.1 = (bf16[4,128,128]{2,1,0:T(8,128)(2,1)S(1)}, bf16[4,128,128]{2,1,0:T(8,128)(2,1)S(1)}, u32[]{:S(2)}, u32[]{:S(2)}) collective-permute-start(bf16[4,128,128]{2,1,0:T(8,128)(2,1)S(1)} %get-tuple-element.16.refs_0_), channel_id=1, source_target_pairs={{0,4},{1,5},{2,6},{3,7},{4,0},{5,1},{6,2},{7,3},{8,12},{9,13},{10,... | collective-permute-start | bytes 393224 | tf_op jit(solution)/shard_map/ppermute | solution.py:20
  20.3 6.7 %collective-permute-start.6 = (bf16[8,128,128]{2,1,0:T(8,128)(2,1)}, bf16[8,128,128]{2,1,0:T(8,128)(2,1)}, u32[]{:S(2)}, u32[]{:S(2)}) collective-permute-start(bf16[8,128,128]{2,1,0:T(8,128)(2,1)} %get-tuple-element.13), channel_id=1, source_target_pairs={{0,32},{16,48},{32,0},{48,16},{64,96},{80,112},{96,64},{112,80},{1... | collective-permute-start | bytes 786440 | tf_op jit(solution)/shard_map/ppermute | solution.py:24
  22.9 3.8 %copy-start.5 = (bf16[8,128,128]{2,1,0:T(8,128)(2,1)S(1)}, bf16[8,128,128]{2,1,0:T(8,128)(2,1)}, u32[]{:S(2)}) copy-start(bf16[8,128,128]{2,1,0:T(8,128)(2,1)} %get-tuple-element.14) | copy-start | bytes 786436
  22.9 4.2 %copy-start.4 = (bf16[2,128,128]{2,1,0:T(8,128)(2,1)S(1)}, bf16[2,128,128]{2,1,0:T(8,128)(2,1)}, u32[]{:S(2)}) copy-start(bf16[2,128,128]{2,1,0:T(8,128)(2,1)} %copy-done.3) | copy-start | bytes 196612
  26.7 7.5 %collective-permute-start.2 = (bf16[8,128,128]{2,1,0:T(8,128)(2,1)S(1)}, bf16[8,128,128]{2,1,0:T(8,128)(2,1)S(1)}, u32[]{:S(2)}, u32[]{:S(2)}) collective-permute-start(bf16[8,128,128]{2,1,0:T(8,128)(2,1)S(1)} %copy-done.5), channel_id=1, source_target_pairs={{0,2},{1,3},{2,0},{3,1},{4,6},{5,7},{6,4},{7,5},{8,10},{9,11},{10,... | collective-permute-start | bytes 786440 | tf_op jit(solution)/shard_map/ppermute | solution.py:20
  28.1 13.5 %collective-permute-start.7 = (bf16[16,128,128]{2,1,0:T(8,128)(2,1)S(1)}, bf16[16,128,128]{2,1,0:T(8,128)(2,1)S(1)}, u32[]{:S(2)}, u32[]{:S(2)}) collective-permute-start(bf16[16,128,128]{2,1,0:T(8,128)(2,1)S(1)} %pad_maximum_fusion.m_ref), channel_id=1, source_target_pairs={{0,1},{1,0},{2,3},{3,2},{4,5},{5,4},{6,7},{7,6},{8,9},{9,8},{10,11... | collective-permute-start | bytes 1572872 | tf_op jit(solution)/shard_map/ppermute | solution.py:20
  50.8 9.8 %collective-permute-start.8 = (bf16[8,128,128]{2,1,0:T(8,128)(2,1)S(1)}, bf16[8,128,128]{2,1,0:T(8,128)(2,1)S(1)}, u32[]{:S(2)}, u32[]{:S(2)}) collective-permute-start(bf16[8,128,128]{2,1,0:T(8,128)(2,1)S(1)} %get-tuple-element.12), channel_id=1, source_target_pairs={{0,2},{1,3},{2,0},{3,1},{4,6},{5,7},{6,4},{7,5},{8,10},{9,11},{10,... | collective-permute-start | bytes 786440 | tf_op jit(solution)/shard_map/ppermute | solution.py:20
  60.7 8.4 %copy-start.7 = (f32[128]{0:T(128)S(1)}, f32[128]{0:T(128)}, u32[]{:S(2)}) copy-start(f32[128]{0:T(128)} %param.11) | copy-start | bytes 1540
  60.7 8.5 %copy-start.8 = (f32[16]{0:T(128)S(1)}, f32[16]{0:T(128)}, u32[]{:S(2)}) copy-start(f32[16]{0:T(128)} %param.10) | copy-start | bytes 196
  60.8 10.4 %copy-start.6 = (bf16[2,1,128,128]{3,2,1,0:T(8,128)(2,1)S(1)}, bf16[2,1,128,128]{3,2,1,0:T(8,128)(2,1)}, u32[]{:S(2)}) copy-start(bf16[2,1,128,128]{3,2,1,0:T(8,128)(2,1)} %param.8) | copy-start | bytes 196612
  60.8 5.6 %collective-permute-start.9 = (bf16[4,128,128]{2,1,0:T(8,128)(2,1)S(1)}, bf16[4,128,128]{2,1,0:T(8,128)(2,1)S(1)}, u32[]{:S(2)}, u32[]{:S(2)}) collective-permute-start(bf16[4,128,128]{2,1,0:T(8,128)(2,1)S(1)} %fusion.2), channel_id=1, source_target_pairs={{0,4},{1,5},{2,6},{3,7},{4,0},{5,1},{6,2},{7,3},{8,12},{9,13},{10,... | collective-permute-start | bytes 393224 | tf_op jit(solution)/shard_map/ppermute | solution.py:20
  66.4 4.7 %collective-permute-start.10 = (bf16[2,128,128]{2,1,0:T(8,128)(2,1)S(1)}, bf16[2,128,128]{2,1,0:T(8,128)(2,1)S(1)}, u32[]{:S(2)}, u32[]{:S(2)}) collective-permute-start(bf16[2,128,128]{2,1,0:T(8,128)(2,1)S(1)} %slice.35), channel_id=1, source_target_pairs={{0,8},{1,9},{2,10},{3,11},{4,12},{5,13},{6,14},{7,15},{8,0},{9,1},... | collective-permute-start | bytes 196616 | tf_op jit(solution)/shard_map/ppermute | solution.py:20
where the time goes:
time: 73.9 us; the launch traced here: 72.5 us
  Pallas kernels  35.6 us (48%)
  starting transfers between devices  22.1 us (30%)
  waiting for transfers between devices  6.06 us (8%)
  other arithmetic  5.99 us (8%)
  local copies, waits for them, and re-layouts  2.51 us (3%)
    pallas_call x7, Pallas kernels, ladder(): pl.pallas_call(kern, in_specs=[VMEM, ANY if fetch else VMEM] + [VMEM] * n...  34 us
    ppermute x8, starting transfers between devices, col_swap(): return lax.ppermute(x, 'col', [(c, c ^ mask) for c in range(16)])  14.8 us
    ppermute x3, starting transfers between devices, row_swap(): return lax.ppermute(x, 'row', [(r, r ^ mask) for r in range(8)])  7.27 us
    ppermute x8, waiting for transfers between devices, col_swap(): return lax.ppermute(x, 'col', [(c, c ^ mask) for c in range(16)])  4.67 us
    concatenate x1, other arithmetic, body(): four_rows = jnp.concatenate([two_rows, rows2])  1.8 us
    concatenate x1, other arithmetic, body(): two_rows = jnp.concatenate([own, rows1])  1.51 us
  transfers between devices with their start and end apart: 11, of which 4 were waited for; matrix products, arithmetic and copies ran while one was open for 10% of the time, Pallas kernels for 37%

commit v1 on v0

--- a/solution.py
+++ b/solution.py
@@ -11,9 +11,8 @@
 F32 = jnp.float32
 VMEM = pl.BlockSpec(memory_space=pltpu.VMEM)
 SMEM = pl.BlockSpec(memory_space=pltpu.SMEM)
-ANY = pl.BlockSpec(memory_space=pl.ANY)
-CHUNK = 8
-PARTS = 4
+HBM = pl.BlockSpec(memory_space=pltpu.HBM)
+PARTS = 8
 
 
 def col_swap(x, mask):
@@ -24,7 +23,7 @@
     return lax.ppermute(x, "row", [(r, r ^ mask) for r in range(8)])
 
 
-def params(mib=48):
+def params(mib):
     return pltpu.CompilerParams(vmem_limit_bytes=mib * 2**20)
 
 
@@ -32,22 +31,21 @@
     return pl.CostEstimate(flops=flops, bytes_accessed=nbytes, transcendentals=0)
 
 
-def ladder(amps, slabs, starts, fetch=False, kind=F32):
-    pairs = amps.shape[0]
+def ladder(amps, slabs, starts, pairs, at=0, fetch=False, give=False, kind=F32, chunk=8):
     duos = pairs // 2
     nq = slabs.shape[0]
-    half = CHUNK // 2
-    steps = nq // CHUNK
+    half = chunk // 2
+    steps = nq // chunk
     nstart = len(starts)
     part = nq // PARTS
-    offsets = [at for _, at in starts]
+    offsets = [n for _, n in starts]
 
     def kern(*refs):
         refs = list(refs)
         t_ref, src_ref = refs[:2]
         s_refs, refs = refs[2 : 2 + nstart], refs[2 + nstart :]
         o_ref = refs.pop(0)
-        b_ref = refs.pop(0) if fetch else src_ref
+        b_ref = refs.pop(0) if give else refs[4] if fetch else src_ref
         xa, xb, acc_ref = refs[:3]
         copies = []
         if fetch:
@@ -60,16 +58,16 @@
             cols = slice((p % 2) * V, (p % 2 + 1) * V)
             if nstart:
                 value = s_refs[0][offsets[0] + p]
-                for ref, at in zip(s_refs[1:], offsets[1:]):
-                    value = value + ref[at + p]
+                for ref, n in zip(s_refs[1:], offsets[1:]):
+                    value = value + ref[n + p]
             else:
                 value = jnp.zeros((V, V), F32)
             acc_ref[p // 2, :, cols] = value
 
         def first(k, q, x_ref):
-            two = b_ref[pl.ds(k * CHUNK + 2 * q, 2)].reshape(2 * V, V)
+            two = b_ref[pl.ds(k * chunk + 2 * q, 2)].reshape(2 * V, V)
             x = lax.dot_general(
-                t_ref[...].reshape(pairs * V, V),
+                t_ref[at : at + pairs].reshape(pairs * V, V),
                 two,
                 (((1,), (1,)), ((), ())),
                 preferred_element_type=F32,
@@ -81,7 +79,7 @@
                 x_ref[g, (2 * q + 1) * V : (2 * q + 2) * V, h * V : (h + 1) * V] = xp[:, V:]
 
         def second(k, g, x_ref):
-            wide = jnp.concatenate([b_ref[k * CHUNK + q] for q in range(CHUNK)], axis=1)
+            wide = jnp.concatenate([b_ref[k * chunk + q] for q in range(chunk)], axis=1)
             acc_ref[g] += jnp.dot(wide, x_ref[g], preferred_element_type=F32)
 
         def both(k1, x1, k2, x2):
@@ -92,13 +90,13 @@
                 for g in range(i * duos // n, (i + 1) * duos // n):
                     second(k2, g, x2)
 
-        if fetch:
-            copies[0].wait()
+        ahead = max(1, chunk // part)
+        for copy in copies[:ahead]:
+            copy.wait()
         for q in range(half):
             first(0, q, xa)
-        if fetch:
-            for copy in copies[1:]:
-                copy.wait()
+        for copy in copies[ahead:]:
+            copy.wait()
 
         def step(m, carry):
             both(2 * m + 1, xb, 2 * m, xa)
@@ -113,20 +111,24 @@
             o_ref[p] = acc_ref[p // 2, :, (p % 2) * V : (p % 2 + 1) * V].astype(kind)
 
     shapes = [jax.ShapeDtypeStruct((pairs, V, V), kind)]
-    scratch = [pltpu.VMEM((duos, CHUNK * V, 2 * V), BF)] * 2 + [pltpu.VMEM((duos, V, 2 * V), F32)]
+    scratch = [pltpu.VMEM((duos, chunk * V, 2 * V), BF)] * 2 + [pltpu.VMEM((duos, V, 2 * V), F32)]
     if fetch:
+        slabs = pltpu.with_memory_space_constraint(slabs, pltpu.HBM)
+        scratch.append(pltpu.SemaphoreType.DMA((PARTS,)))
+    if give:
         shapes.append(jax.ShapeDtypeStruct(slabs.shape, BF))
-        scratch.append(pltpu.SemaphoreType.DMA((PARTS,)))
+    elif fetch:
+        scratch.append(pltpu.VMEM(slabs.shape, BF))
     out = pl.pallas_call(
         kern,
-        in_specs=[VMEM, ANY if fetch else VMEM] + [VMEM] * nstart,
+        in_specs=[VMEM, HBM if fetch else VMEM] + [VMEM] * nstart,
         out_specs=[VMEM] * len(shapes),
         out_shape=shapes,
         scratch_shapes=scratch,
-        compiler_params=params(),
+        compiler_params=params(8 + duos * chunk * 256 // 1024),
         cost_estimate=cost(4 * pairs * nq * V**3, slabs.size * 2),
     )(amps, slabs, *[s for s, _ in starts])
-    return out if fetch else out[0]
+    return out if give else out[0]
 
 
 def spread_ints(ints, where):
@@ -152,7 +154,7 @@
         in_specs=[SMEM, VMEM],
         out_specs=VMEM,
         out_shape=jax.ShapeDtypeStruct((256, 512), BF),
-        compiler_params=params(),
+        compiler_params=params(8),
         cost_estimate=cost(10**8, 10**6),
         name="spread",
     )(where, ints)
@@ -175,7 +177,7 @@
         in_specs=[VMEM] * 3,
         out_specs=VMEM,
         out_shape=jax.ShapeDtypeStruct((16, V, V), F32),
-        compiler_params=params(),
+        compiler_params=params(8),
         cost_estimate=cost(10**9, 10**6),
         name="hole",
     )(wide, mine, other)
@@ -191,27 +193,31 @@
     rows1 = row_swap(own, 1)
     ints = lax.dynamic_slice_in_dim(hole_ints, r * 2, 2, 0).reshape(32, 256)
     wide = spread_ints(ints, where)
-    part_0, slabs = ladder(own, df_slabs, [], True)
+    part_0 = ladder(own, df_slabs, [], 2, fetch=True)
     near = jnp.concatenate([own, got_y2])
     got_y1 = col_swap(near, 4)
     two_rows = jnp.concatenate([own, rows1])
     rows2 = row_swap(two_rows, 4)
-    part_4 = ladder(got_y2, slabs, [])
+    part_4 = ladder(got_y2, df_slabs, [], 2, fetch=True)
     got_x = col_swap(jnp.concatenate([near, got_y1]), 2)
     four_rows = jnp.concatenate([two_rows, rows2])
     rows3 = row_swap(four_rows, 2)
-    part_26 = ladder(got_y1, slabs, [])
+    part_26 = ladder(got_y1, df_slabs, [], 4, fetch=True)
     mine = jnp.concatenate([four_rows, rows3])
     other = col_swap(mine, 1)
-    part_x = ladder(got_x, slabs, [])
+    part_x = ladder(got_x, df_slabs, [], 8, fetch=True, chunk=16)
     hole = hole_terms(wide, mine, other)
-    send_x, fetched = ladder(got_x, others, [(part_x, 0), (hole, 8)], True, BF)
-    back_x = col_swap(send_x, 2).astype(F32)
-    full_26 = ladder(got_y1, fetched, [(part_26, 0), (hole, 4)])
-    back_y1 = col_swap((full_26 + back_x[4:]).astype(BF), 4).astype(F32)
+    send_b, fetched = ladder(
+        got_x, others, [(part_x, 4), (hole, 12)], 4, 4, fetch=True, give=True, kind=BF
+    )
+    back_b = col_swap(send_b, 2).astype(F32)
+    send_a = ladder(got_x, fetched, [(part_x, 0), (hole, 8)], 4, 0, kind=BF)
+    back_a = col_swap(send_a, 2).astype(F32)
+    full_26 = ladder(got_y1, fetched, [(part_26, 0), (hole, 4)], 4)
+    back_y1 = col_swap((full_26 + back_b).astype(BF), 4).astype(F32)
     start_04 = jnp.concatenate([part_0, part_4])
-    full_04 = ladder(near, fetched, [(start_04, 0), (hole, 0)])
-    total = full_04 + back_x[:4] + back_y1
+    full_04 = ladder(near, fetched, [(start_04, 0), (hole, 0)], 4)
+    total = full_04 + back_a + back_y1
     back_y2 = col_swap(total[2:].astype(BF), 8).astype(F32)
     total = total[:2] + back_y2
     occ_first = lax.dynamic_slice_in_dim(eps_occ, r * 2, 2, 0)

time: 73.9 us -> 78 us (1.055)
  Pallas kernels: 35.6 us -> 40.9 us
  waiting for transfers between devices: 6.06 us -> 9.91 us
  other arithmetic: 5.99 us -> 3.35 us
  starting transfers between devices: 22.1 us -> 20.6 us
  local copies, waits for them, and re-layouts: 2.51 us -> 1.71 us
    pallas_call x7 -> x8, Pallas kernels: 34 us -> 39.4 us  [ladder(): pl.pallas_call(kern, in_specs=[VMEM, HBM if fetch else VMEM] + [VMEM] * n...]
    ppermute x3, waiting for transfers between devices: 1.39 us -> 4.34 us  [row_swap(): return lax.ppermute(x, 'row', [(r, r ^ mask) for r in range(8)])]
    ppermute x8 -> x9, starting transfers between devices: 14.8 us -> 13.2 us  [col_swap(): return lax.ppermute(x, 'col', [(c, c ^ mask) for c in range(16)])]
    concatenate x1, other arithmetic: 1.04 us -> 0.05 us  [body(): mine = jnp.concatenate([four_rows, rows3])]
    concatenate x1, other arithmetic: 1.8 us -> 0.88 us  [body(): four_rows = jnp.concatenate([two_rows, rows2])]
    reshape x1, local copies, waits for them, and re-layouts: 1.06 us -> 0.16 us  [body(): ints = lax.dynamic_slice_in_dim(hole_ints, r * 2, 2, 0).reshape(32, 256)]
    ppermute x8 -> x9, waiting for transfers between devices: 4.67 us -> 5.57 us  [col_swap(): return lax.ppermute(x, 'col', [(c, c ^ mask) for c in range(16)])]
    unnamed x18 -> x12, local copies, waits for them, and re-layouts: 0.04 us -> 0.87 us
  transfers between devices with their start and end apart: 11 -> 12, of which waited for: 4 -> 4; matrix products, arithmetic and copies ran while one was open for 10% -> 4% of each run, Pallas kernels for 37% -> 41%
where the time goes in v1:
time: 78 us; the launch traced here: 76.7 us
  Pallas kernels  40.9 us (52%)
  starting transfers between devices  20.6 us (26%)
  waiting for transfers between devices  9.91 us (13%)
  other arithmetic  3.35 us (4%)
  local copies, waits for them, and re-layouts  1.71 us (2%)
    pallas_call x8, Pallas kernels, ladder(): pl.pallas_call(kern, in_specs=[VMEM, HBM if fetch else VMEM] + [VMEM] * n...  39.4 us
    ppermute x9, starting transfers between devices, col_swap(): return lax.ppermute(x, 'col', [(c, c ^ mask) for c in range(16)])  13.2 us
    ppermute x3, starting transfers between devices, row_swap(): return lax.ppermute(x, 'row', [(r, r ^ mask) for r in range(8)])  7.43 us
    ppermute x9, waiting for transfers between devices, col_swap(): return lax.ppermute(x, 'col', [(c, c ^ mask) for c in range(16)])  5.57 us
    ppermute x3, waiting for transfers between devices, row_swap(): return lax.ppermute(x, 'row', [(r, r ^ mask) for r in range(8)])  4.34 us
  transfers between devices with their start and end apart: 12, of which 4 were waited for; matrix products, arithmetic and copies ran while one was open for 4% of the time, Pallas kernels for 41%

profile of v1, /device:TPU:1, one launch (start us, length us, event | category | flops | bytes accessed | tf_op | source)
XLA Modules:
  0.0 76.7 jit_solution(12533460430534542472)
XLA Ops:
  0.0 1.4 %collective-permute-start.3 = (bf16[64,128,128]{2,1,0:T(8,128)(2,1)}, bf16[64,128,128]{2,1,0:T(8,128)(2,1)}, u32[]{:S(2)}, u32[]{:S(2)}) collective-permute-start(bf16[64,128,128]{2,1,0:T(8,128)(2,1)} %refs_1_.7), channel_id=1, source_target_pairs={{0,1},{1,0},{2,3},{3,2},{4,5},{5,4},{6,7},{7,6},{8,9},{9,8},{10,11... | collective-permute-start | bytes 6291464 | tf_op jit(solution)/shard_map/ppermute | solution.py:19
  1.4 3.0 %collective-permute-start = (bf16[2,128,128]{2,1,0:T(8,128)(2,1)}, bf16[2,128,128]{2,1,0:T(8,128)(2,1)S(1)}, u32[]{:S(2)}, u32[]{:S(2)}) collective-permute-start(bf16[2,128,128]{2,1,0:T(8,128)(2,1)} %bitcast.15), channel_id=1, source_target_pairs={{0,8},{1,9},{2,10},{3,11},{4,12},{5,13},{6,14},{7,15},{8,0},{9,1},... | collective-permute-start | bytes 196616 | tf_op jit(solution)/shard_map/ppermute | solution.py:19
  4.4 2.7 %collective-permute-start.4 = (bf16[2,128,128]{2,1,0:T(8,128)(2,1)}, bf16[2,128,128]{2,1,0:T(8,128)(2,1)S(1)}, u32[]{:S(2)}, u32[]{:S(2)}) collective-permute-start(bf16[2,128,128]{2,1,0:T(8,128)(2,1)} %bitcast.16), channel_id=1, source_target_pairs={{0,16},{16,0},{32,48},{48,32},{64,80},{80,64},{96,112},{112,96},{1... | collective-permute-start | bytes 196616 | tf_op jit(solution)/shard_map/ppermute | solution.py:23
  7.2 2.1 %collective-permute-done.4 = bf16[2,128,128]{2,1,0:T(8,128)(2,1)S(1)} collective-permute-done((bf16[2,128,128]{2,1,0:T(8,128)(2,1)}, bf16[2,128,128]{2,1,0:T(8,128)(2,1)S(1)}, u32[]{:S(2)}, u32[]{:S(2)}) %collective-permute-start.4) | collective-permute-done | bytes 65568 | tf_op jit(solution)/shard_map/ppermute | solution.py:23
  10.6 3.6 %collective-permute-start.5 = (bf16[4,128,128]{2,1,0:T(8,128)(2,1)S(1)}, bf16[4,128,128]{2,1,0:T(8,128)(2,1)S(1)}, u32[]{:S(2)}, u32[]{:S(2)}) collective-permute-start(bf16[4,128,128]{2,1,0:T(8,128)(2,1)S(1)} %get-tuple-element.11), channel_id=1, source_target_pairs={{0,64},{16,80},{32,96},{48,112},{64,0},{80,16},{96,32},{112,48},{1... | collective-permute-start | bytes 393224 | tf_op jit(solution)/shard_map/ppermute | solution.py:23
  14.3 2.3 %collective-permute-done.5 = bf16[4,128,128]{2,1,0:T(8,128)(2,1)S(1)} collective-permute-done((bf16[4,128,128]{2,1,0:T(8,128)(2,1)S(1)}, bf16[4,128,128]{2,1,0:T(8,128)(2,1)S(1)}, u32[]{:S(2)}, u32[]{:S(2)}) %collective-permute-start.5) | collective-permute-done | bytes 131104 | tf_op jit(solution)/shard_map/ppermute | solution.py:23
  16.5 0.9 %fusion.1 = (bf16[8,128,128]{2,1,0:T(8,128)(2,1)S(1)}, bf16[8,128,128]{2,1,0:T(8,128)(2,1)S(1)}) fusion(bf16[2,128,128]{2,1,0:T(8,128)(2,1)} %bitcast.18, bf16[4,128,128]{2,1,0:T(8,128)(2,1)S(1)} %collective-permute-done.5, bf16[2,128,128]{2,1,0:T(8,128)(2,1)S(1)} %collective-permute-done.4, bf16[4,128,128]{2,1,0:T(8,128)(2,1)S(1)} %collective-permute-done.1.refs_0_, ...), kind=kLoop, calls=%fused_computation.4 | loop fusion | flops 524288 | bytes 983040 | tf_op jit(solution)/shard_map/concatenate | solution.py:203
  17.4 1.1 %collective-permute-start.6 = (bf16[8,128,128]{2,1,0:T(8,128)(2,1)S(1)}, bf16[8,128,128]{2,1,0:T(8,128)(2,1)S(1)}, u32[]{:S(2)}, u32[]{:S(2)}) collective-permute-start(bf16[8,128,128]{2,1,0:T(8,128)(2,1)S(1)} %get-tuple-element.9), channel_id=1, source_target_pairs={{0,32},{16,48},{32,0},{48,16},{64,96},{80,112},{96,64},{112,80},{1... | collective-permute-start | bytes 786440 | tf_op jit(solution)/shard_map/ppermute | solution.py:23
  19.4 4.0 %shard_map.66 = f32[2,128,128]{2,1,0:T(8,128)S(1)} custom-call(bf16[2,128,128]{2,1,0:T(8,128)(2,1)S(1)} %bitcast.19, bf16[64,128,128]{2,1,0:T(8,128)(2,1)} %refs_1_.7), custom_call_target="tpu_custom_call" | custom-call | flops 1073741824 | bytes 2097152 | tf_op jit(solution)/shard_map/pallas_call | solution.py:122
  23.5 0.9 %spread.1.w_ref = bf16[256,512]{1,0:T(8,128)(2,1)S(1)} custom-call(s32[2]{0:T(128)S(1)} %pad_add_fusion.w_ref, bf16[32,256]{1,0:T(8,128)(2,1)S(1)} %reshape.47.h_ref), custom_call_target="tpu_custom_call" | custom-call | flops 100000000 | bytes 1000000 | tf_op jit(solution)/shard_map/spread/pallas_call | solution.py:152
  24.4 4.0 %shard_map.67 = f32[2,128,128]{2,1,0:T(8,128)S(1)} custom-call(bf16[2,128,128]{2,1,0:T(8,128)(2,1)S(1)} %collective-permute-done.refs_0_, bf16[64,128,128]{2,1,0:T(8,128)(2,1)} %refs_1_.7), custom_call_target="tpu_custom_call" | custom-call | flops 1073741824 | bytes 2097152 | tf_op jit(solution)/shard_map/pallas_call | solution.py:122
  28.4 1.3 %collective-permute-start.2 = (bf16[8,128,128]{2,1,0:T(8,128)(2,1)S(1)}, bf16[8,128,128]{2,1,0:T(8,128)(2,1)S(1)}, u32[]{:S(2)}, u32[]{:S(2)}) collective-permute-start(bf16[8,128,128]{2,1,0:T(8,128)(2,1)S(1)} %get-tuple-element.10), channel_id=1, source_target_pairs={{0,2},{1,3},{2,0},{3,1},{4,6},{5,7},{6,4},{7,5},{8,10},{9,11},{10,... | collective-permute-start | bytes 786440 | tf_op jit(solution)/shard_map/ppermute | solution.py:19
  29.8 3.8 %collective-permute-start.7 = (bf16[16,128,128]{2,1,0:T(8,128)(2,1)S(1)}, bf16[16,128,128]{2,1,0:T(8,128)(2,1)S(1)}, u32[]{:S(2)}, u32[]{:S(2)}) collective-permute-start(bf16[16,128,128]{2,1,0:T(8,128)(2,1)S(1)} %pad_maximum_fusion.m_ref), channel_id=1, source_target_pairs={{0,1},{1,0},{2,3},{3,2},{4,5},{5,4},{6,7},{7,6},{8,9},{9,8},{10,11... | collective-permute-start | bytes 1572872 | tf_op jit(solution)/shard_map/ppermute | solution.py:19
  33.5 5.3 %shard_map.70.refs_2_ = f32[4,128,128]{2,1,0:T(8,128)S(1)} custom-call(bf16[4,128,128]{2,1,0:T(8,128)(2,1)S(1)} %collective-permute-done.1.refs_0_, bf16[64,128,128]{2,1,0:T(8,128)(2,1)} %refs_1_.7), custom_call_target="tpu_custom_call" | custom-call | flops 2147483648 | bytes 2097152 | tf_op jit(solution)/shard_map/pallas_call | solution.py:122
  38.9 8.0 %shard_map.64.refs_2_ = f32[8,128,128]{2,1,0:T(8,128)S(1)} custom-call(bf16[8,128,128]{2,1,0:T(8,128)(2,1)S(1)} %collective-permute-done.2.refs_0_, bf16[64,128,128]{2,1,0:T(8,128)(2,1)} %refs_1_.7), custom_call_target="tpu_custom_call" | custom-call | flops 4294967296 | bytes 2097152 | tf_op jit(solution)/shard_map/pallas_call | solution.py:122
  47.6 5.3 %shard_map.65 = (bf16[4,128,128]{2,1,0:T(8,128)(2,1)S(1)}, bf16[64,128,128]{2,1,0:T(8,128)(2,1)S(1)}) custom-call(bf16[8,128,128]{2,1,0:T(8,128)(2,1)S(1)} %collective-permute-done.2.refs_0_, bf16[64,128,128]{2,1,0:T(8,128)(2,1)} %collective-permute-done.3.refs_1_, f32[8,128,128]{2,1,0:T(8,128)S(1)} %shard_map.64.refs_2_, f32[16,128,128]{2,1,0:T(8,128)S(1)} %hole.1.refs_3_), custom_call_target="tpu_custom_call" | custom-call | flops 2147483648 | bytes 2097152 | tf_op jit(solution)/shard_map/pallas_call | solution.py:122
  52.9 4.4 %shard_map.69 = bf16[4,128,128]{2,1,0:T(8,128)(2,1)S(1)} custom-call(bf16[8,128,128]{2,1,0:T(8,128)(2,1)S(1)} %collective-permute-done.2.refs_0_, bf16[64,128,128]{2,1,0:T(8,128)(2,1)S(1)} %get-tuple-element.7.refs_1_, f32[8,128,128]{2,1,0:T(8,128)S(1)} %shard_map.64.refs_2_, f32[16,128,128]{2,1,0:T(8,128)S(1)} %hole.1.refs_3_), custom_call_target="tpu_custom_call" | custom-call | flops 2147483648 | bytes 2097152 | tf_op jit(solution)/shard_map/pallas_call | solution.py:122
  57.6 1.2 %collective-permute-start.9 = (bf16[4,128,128]{2,1,0:T(8,128)(2,1)S(1)}, bf16[4,128,128]{2,1,0:T(8,128)(2,1)S(1)}, u32[]{:S(2)}, u32[]{:S(2)}) collective-permute-start(bf16[4,128,128]{2,1,0:T(8,128)(2,1)S(1)} %get-tuple-element.8), channel_id=1, source_target_pairs={{0,2},{1,3},{2,0},{3,1},{4,6},{5,7},{6,4},{7,5},{8,10},{9,11},{10,... | collective-permute-start | bytes 393224 | tf_op jit(solution)/shard_map/ppermute | solution.py:19
  58.9 4.2 %shard_map.71 = f32[4,128,128]{2,1,0:T(8,128)S(1)} custom-call(bf16[4,128,128]{2,1,0:T(8,128)(2,1)S(1)} %collective-permute-done.1.refs_0_, bf16[64,128,128]{2,1,0:T(8,128)(2,1)S(1)} %get-tuple-element.7.refs_1_, f32[4,128,128]{2,1,0:T(8,128)S(1)} %shard_map.70.refs_2_, f32[16,128,128]{2,1,0:T(8,128)S(1)} %hole.1.refs_3_), custom_call_target="tpu_custom_call" | custom-call | flops 2147483648 | bytes 2097152 | tf_op jit(solution)/shard_map/pallas_call | solution.py:122
  63.0 2.2 %collective-permute-done.9 = bf16[4,128,128]{2,1,0:T(8,128)(2,1)S(1)} collective-permute-done((bf16[4,128,128]{2,1,0:T(8,128)(2,1)S(1)}, bf16[4,128,128]{2,1,0:T(8,128)(2,1)S(1)}, u32[]{:S(2)}, u32[]{:S(2)}) %collective-permute-start.9) | collective-permute-done | bytes 131104 | tf_op jit(solution)/shard_map/ppermute | solution.py:19
  65.3 1.1 %collective-permute-start.10 = (bf16[4,128,128]{2,1,0:T(8,128)(2,1)S(1)}, bf16[4,128,128]{2,1,0:T(8,128)(2,1)S(1)}, u32[]{:S(2)}, u32[]{:S(2)}) collective-permute-start(bf16[4,128,128]{2,1,0:T(8,128)(2,1)S(1)} %add_convert_fusion), channel_id=1, source_target_pairs={{0,4},{1,5},{2,6},{3,7},{4,0},{5,1},{6,2},{7,3},{8,12},{9,13},{10,... | collective-permute-start | bytes 393224 | tf_op jit(solution)/shard_map/ppermute | solution.py:19
  66.5 4.2 %shard_map.68 = f32[4,128,128]{2,1,0:T(8,128)S(1)} custom-call(bf16[4,128,128]{2,1,0:T(8,128)(2,1)S(1)} %get-tuple-element.12.refs_0_, bf16[64,128,128]{2,1,0:T(8,128)(2,1)S(1)} %get-tuple-element.7.refs_1_, f32[4,128,128]{2,1,0:T(8,128)S(1)} %pad_maximum_fusion.3.refs_2_, f32[16,128,128]{2,1,0:T(8,128)S(1)} %hole.1.refs_3_), custom_call_target="tpu_custom_call" | custom-call | flops 2147483648 | bytes 2097152 | tf_op jit(solution)/shard_map/pallas_call | solution.py:122
  72.1 3.4 %collective-permute-done.11 = bf16[2,128,128]{2,1,0:T(8,128)(2,1)S(1)} collective-permute-done((bf16[2,128,128]{2,1,0:T(8,128)(2,1)S(1)}, bf16[2,128,128]{2,1,0:T(8,128)(2,1)S(1)}, u32[]{:S(2)}, u32[]{:S(2)}) %collective-permute-start.11) | collective-permute-done | bytes 65568 | tf_op jit(solution)/shard_map/ppermute | solution.py:19
  75.4 1.3 %fusion.4 = f32[2,1,128,128]{3,2,1,0:T(8,128)} fusion(f32[4,128,128]{2,1,0:T(8,128)S(1)} %convert_add_fusion, bf16[2,128,128]{2,1,0:T(8,128)(2,1)S(1)} %collective-permute-done.11, bf16[2,1,128,128]{3,2,1,0:T(8,128)(2,1)S(1)} %copy-done.3, f32[]{:T(128)} %bitcast.5, f32[2]{0:T(128)S(1)} %dynamic_slice.10, f32[128,128]{1,0:T(8,128)S(1)} %broadcast_add_fusion), kind=kLoop, calls=%fused_computation.14 | loop fusion | flops 229376 | bytes 458764 | tf_op jit(solution)/shard_map/reshape | solution.py:231
  (36 shorter events, 5.0 us)
Async XLA Ops:
  0.0 14.3 %copy-start = (bf16[16,16,16,16]{3,2,1,0:T(8,128)(2,1)S(1)}, bf16[16,16,16,16]{3,2,1,0:T(8,128)(2,1)}, u32[]{:S(2)}) copy-start(bf16[16,16,16,16]{3,2,1,0:T(8,128)(2,1)} %param.9) | copy-start | bytes 393220
  0.0 47.6 %collective-permute-start.3 = (bf16[64,128,128]{2,1,0:T(8,128)(2,1)}, bf16[64,128,128]{2,1,0:T(8,128)(2,1)}, u32[]{:S(2)}, u32[]{:S(2)}) collective-permute-start(bf16[64,128,128]{2,1,0:T(8,128)(2,1)} %refs_1_.7), channel_id=1, source_target_pairs={{0,1},{1,0},{2,3},{3,2},{4,5},{5,4},{6,7},{7,6},{8,9},{9,8},{10,11... | collective-permute-start | bytes 6291464 | tf_op jit(solution)/shard_map/ppermute | solution.py:19
  1.4 5.8 %collective-permute-start = (bf16[2,128,128]{2,1,0:T(8,128)(2,1)}, bf16[2,128,128]{2,1,0:T(8,128)(2,1)S(1)}, u32[]{:S(2)}, u32[]{:S(2)}) collective-permute-start(bf16[2,128,128]{2,1,0:T(8,128)(2,1)} %bitcast.15), channel_id=1, source_target_pairs={{0,8},{1,9},{2,10},{3,11},{4,12},{5,13},{6,14},{7,15},{8,0},{9,1},... | collective-permute-start | bytes 196616 | tf_op jit(solution)/shard_map/ppermute | solution.py:19
  4.4 4.8 %collective-permute-start.4 = (bf16[2,128,128]{2,1,0:T(8,128)(2,1)}, bf16[2,128,128]{2,1,0:T(8,128)(2,1)S(1)}, u32[]{:S(2)}, u32[]{:S(2)}) collective-permute-start(bf16[2,128,128]{2,1,0:T(8,128)(2,1)} %bitcast.16), channel_id=1, source_target_pairs={{0,16},{16,0},{32,48},{48,32},{64,80},{80,64},{96,112},{112,96},{1... | collective-permute-start | bytes 196616 | tf_op jit(solution)/shard_map/ppermute | solution.py:23
  10.1 4.2 %collective-permute-start.1 = (bf16[4,128,128]{2,1,0:T(8,128)(2,1)S(1)}, bf16[4,128,128]{2,1,0:T(8,128)(2,1)S(1)}, u32[]{:S(2)}, u32[]{:S(2)}) collective-permute-start(bf16[4,128,128]{2,1,0:T(8,128)(2,1)S(1)} %get-tuple-element.12.refs_0_), channel_id=1, source_target_pairs={{0,4},{1,5},{2,6},{3,7},{4,0},{5,1},{6,2},{7,3},{8,12},{9,13},{10,... | collective-permute-start | bytes 393224 | tf_op jit(solution)/shard_map/ppermute | solution.py:19
  10.6 6.0 %collective-permute-start.5 = (bf16[4,128,128]{2,1,0:T(8,128)(2,1)S(1)}, bf16[4,128,128]{2,1,0:T(8,128)(2,1)S(1)}, u32[]{:S(2)}, u32[]{:S(2)}) collective-permute-start(bf16[4,128,128]{2,1,0:T(8,128)(2,1)S(1)} %get-tuple-element.11), channel_id=1, source_target_pairs={{0,64},{16,80},{32,96},{48,112},{64,0},{80,16},{96,32},{112,48},{1... | collective-permute-start | bytes 393224 | tf_op jit(solution)/shard_map/ppermute | solution.py:23
  17.4 12.3 %collective-permute-start.6 = (bf16[8,128,128]{2,1,0:T(8,128)(2,1)S(1)}, bf16[8,128,128]{2,1,0:T(8,128)(2,1)S(1)}, u32[]{:S(2)}, u32[]{:S(2)}) collective-permute-start(bf16[8,128,128]{2,1,0:T(8,128)(2,1)S(1)} %get-tuple-element.9), channel_id=1, source_target_pairs={{0,32},{16,48},{32,0},{48,16},{64,96},{80,112},{96,64},{112,80},{1... | collective-permute-start | bytes 786440 | tf_op jit(solution)/shard_map/ppermute | solution.py:23
  18.5 0.8 %copy-start.1 = (bf16[2,1,128,128]{3,2,1,0:T(8,128)(2,1)S(1)}, bf16[2,1,128,128]{3,2,1,0:T(8,128)(2,1)}, u32[]{:S(2)}) copy-start(bf16[2,1,128,128]{3,2,1,0:T(8,128)(2,1)} %param.6) | copy-start | bytes 196612
  24.4 5.4 %copy-start.2 = (bf16[2,1,128,128]{3,2,1,0:T(8,128)(2,1)S(1)}, bf16[2,1,128,128]{3,2,1,0:T(8,128)(2,1)}, u32[]{:S(2)}) copy-start(bf16[2,1,128,128]{3,2,1,0:T(8,128)(2,1)} %param.6) | copy-start | bytes 196612
  28.4 10.4 %collective-permute-start.2 = (bf16[8,128,128]{2,1,0:T(8,128)(2,1)S(1)}, bf16[8,128,128]{2,1,0:T(8,128)(2,1)S(1)}, u32[]{:S(2)}, u32[]{:S(2)}) collective-permute-start(bf16[8,128,128]{2,1,0:T(8,128)(2,1)S(1)} %get-tuple-element.10), channel_id=1, source_target_pairs={{0,2},{1,3},{2,0},{3,1},{4,6},{5,7},{6,4},{7,5},{8,10},{9,11},{10,... | collective-permute-start | bytes 786440 | tf_op jit(solution)/shard_map/ppermute | solution.py:19
  29.8 17.1 %collective-permute-start.7 = (bf16[16,128,128]{2,1,0:T(8,128)(2,1)S(1)}, bf16[16,128,128]{2,1,0:T(8,128)(2,1)S(1)}, u32[]{:S(2)}, u32[]{:S(2)}) collective-permute-start(bf16[16,128,128]{2,1,0:T(8,128)(2,1)S(1)} %pad_maximum_fusion.m_ref), channel_id=1, source_target_pairs={{0,1},{1,0},{2,3},{3,2},{4,5},{5,4},{6,7},{7,6},{8,9},{9,8},{10,11... | collective-permute-start | bytes 1572872 | tf_op jit(solution)/shard_map/ppermute | solution.py:19
  57.3 13.3 %collective-permute-start.8 = (bf16[4,128,128]{2,1,0:T(8,128)(2,1)S(1)}, bf16[4,128,128]{2,1,0:T(8,128)(2,1)S(1)}, u32[]{:S(2)}, u32[]{:S(2)}) collective-permute-start(bf16[4,128,128]{2,1,0:T(8,128)(2,1)S(1)} %shard_map.69), channel_id=1, source_target_pairs={{0,2},{1,3},{2,0},{3,1},{4,6},{5,7},{6,4},{7,5},{8,10},{9,11},{10,... | collective-permute-start | bytes 393224 | tf_op jit(solution)/shard_map/ppermute | solution.py:19
  57.6 7.6 %collective-permute-start.9 = (bf16[4,128,128]{2,1,0:T(8,128)(2,1)S(1)}, bf16[4,128,128]{2,1,0:T(8,128)(2,1)S(1)}, u32[]{:S(2)}, u32[]{:S(2)}) collective-permute-start(bf16[4,128,128]{2,1,0:T(8,128)(2,1)S(1)} %get-tuple-element.8), channel_id=1, source_target_pairs={{0,2},{1,3},{2,0},{3,1},{4,6},{5,7},{6,4},{7,5},{8,10},{9,11},{10,... | collective-permute-start | bytes 393224 | tf_op jit(solution)/shard_map/ppermute | solution.py:19
  65.3 6.1 %copy-start.4 = (f32[128]{0:T(128)S(1)}, f32[128]{0:T(128)}, u32[]{:S(2)}) copy-start(f32[128]{0:T(128)} %param.11) | copy-start | bytes 1540
  65.3 6.1 %copy-start.5 = (f32[16]{0:T(128)S(1)}, f32[16]{0:T(128)}, u32[]{:S(2)}) copy-start(f32[16]{0:T(128)} %param.10) | copy-start | bytes 196
  65.3 10.1 %copy-start.3 = (bf16[2,1,128,128]{3,2,1,0:T(8,128)(2,1)S(1)}, bf16[2,1,128,128]{3,2,1,0:T(8,128)(2,1)}, u32[]{:S(2)}) copy-start(bf16[2,1,128,128]{3,2,1,0:T(8,128)(2,1)} %param.8) | copy-start | bytes 196612
  65.3 5.4 %collective-permute-start.10 = (bf16[4,128,128]{2,1,0:T(8,128)(2,1)S(1)}, bf16[4,128,128]{2,1,0:T(8,128)(2,1)S(1)}, u32[]{:S(2)}, u32[]{:S(2)}) collective-permute-start(bf16[4,128,128]{2,1,0:T(8,128)(2,1)S(1)} %add_convert_fusion), channel_id=1, source_target_pairs={{0,4},{1,5},{2,6},{3,7},{4,0},{5,1},{6,2},{7,3},{8,12},{9,13},{10,... | collective-permute-start | bytes 393224 | tf_op jit(solution)/shard_map/ppermute | solution.py:19
  70.7 4.7 %collective-permute-start.11 = (bf16[2,128,128]{2,1,0:T(8,128)(2,1)S(1)}, bf16[2,128,128]{2,1,0:T(8,128)(2,1)S(1)}, u32[]{:S(2)}, u32[]{:S(2)}) collective-permute-start(bf16[2,128,128]{2,1,0:T(8,128)(2,1)S(1)} %slice.19), channel_id=1, source_target_pairs={{0,8},{1,9},{2,10},{3,11},{4,12},{5,13},{6,14},{7,15},{8,0},{9,1},... | collective-permute-start | bytes 196616 | tf_op jit(solution)/shard_map/ppermute | solution.py:19

commit v2 on v1

--- a/solution.py
+++ b/solution.py
@@ -31,43 +31,54 @@
     return pl.CostEstimate(flops=flops, bytes_accessed=nbytes, transcendentals=0)
 
 
-def ladder(amps, slabs, starts, pairs, at=0, fetch=False, give=False, kind=F32, chunk=8):
+def ladder(amps, slabs, starts, pull=False, kind=F32, chunk=8):
+    pairs = sum(n for _, _, n in amps)
     duos = pairs // 2
     nq = slabs.shape[0]
     half = chunk // 2
     steps = nq // chunk
-    nstart = len(starts)
     part = nq // PARTS
-    offsets = [n for _, n in starts]
+    namps = len(amps)
+    nstart = sum(len(pieces) for pieces in starts)
 
     def kern(*refs):
         refs = list(refs)
-        t_ref, src_ref = refs[:2]
-        s_refs, refs = refs[2 : 2 + nstart], refs[2 + nstart :]
+        t_refs, src_ref = refs[:namps], refs[namps]
+        s_refs, refs = refs[namps + 1 : namps + 1 + nstart], refs[namps + 1 + nstart :]
         o_ref = refs.pop(0)
-        b_ref = refs.pop(0) if give else refs[4] if fetch else src_ref
-        xa, xb, acc_ref = refs[:3]
+        b_ref = refs.pop(0) if pull else src_ref
+        xa, xb, acc_ref, home = refs[:4]
         copies = []
-        if fetch:
-            sems = refs[3]
+        if pull:
+            pulled = pltpu.make_async_copy(t_refs[0], home, refs[5])
+            pulled.start()
             for n in range(PARTS):
                 span = pl.ds(n * part, part)
-                copies.append(pltpu.make_async_copy(src_ref.at[span], b_ref.at[span], sems.at[n]))
+                copies.append(pltpu.make_async_copy(src_ref.at[span], b_ref.at[span], refs[4].at[n]))
                 copies[-1].start()
+        else:
+            to = 0
+            for ref, (_, at, n) in zip(t_refs, amps):
+                home[to : to + n] = ref[at : at + n]
+                to += n
+        sums = [None] * pairs
+        left = list(s_refs)
+        for pieces in starts:
+            to = 0
+            for _, at, n in pieces:
+                ref = left.pop(0)
+                for p in range(n):
+                    value = ref[at + p]
+                    sums[to + p] = value if sums[to + p] is None else sums[to + p] + value
+                to += n
         for p in range(pairs):
-            cols = slice((p % 2) * V, (p % 2 + 1) * V)
-            if nstart:
-                value = s_refs[0][offsets[0] + p]
-                for ref, n in zip(s_refs[1:], offsets[1:]):
-                    value = value + ref[n + p]
-            else:
-                value = jnp.zeros((V, V), F32)
-            acc_ref[p // 2, :, cols] = value
+            value = jnp.zeros((V, V), F32) if sums[p] is None else sums[p]
+            acc_ref[p // 2, :, (p % 2) * V : (p % 2 + 1) * V] = value
 
         def first(k, q, x_ref):
             two = b_ref[pl.ds(k * chunk + 2 * q, 2)].reshape(2 * V, V)
             x = lax.dot_general(
-                t_ref[at : at + pairs].reshape(pairs * V, V),
+                home[...].reshape(pairs * V, V),
                 two,
                 (((1,), (1,)), ((), ())),
                 preferred_element_type=F32,
@@ -90,6 +101,8 @@
                 for g in range(i * duos // n, (i + 1) * duos // n):
                     second(k2, g, x2)
 
+        if pull:
+            pulled.wait()
         ahead = max(1, chunk // part)
         for copy in copies[:ahead]:
             copy.wait()
@@ -112,23 +125,23 @@
 
     shapes = [jax.ShapeDtypeStruct((pairs, V, V), kind)]
     scratch = [pltpu.VMEM((duos, chunk * V, 2 * V), BF)] * 2 + [pltpu.VMEM((duos, V, 2 * V), F32)]
-    if fetch:
-        slabs = pltpu.with_memory_space_constraint(slabs, pltpu.HBM)
-        scratch.append(pltpu.SemaphoreType.DMA((PARTS,)))
-    if give:
+    scratch.append(pltpu.VMEM((pairs, V, V), BF))
+    arrays = [array for array, _, _ in amps] + [slabs]
+    if pull:
         shapes.append(jax.ShapeDtypeStruct(slabs.shape, BF))
-    elif fetch:
-        scratch.append(pltpu.VMEM(slabs.shape, BF))
+        scratch += [pltpu.SemaphoreType.DMA((PARTS,)), pltpu.SemaphoreType.DMA(())]
+        arrays = [pltpu.with_memory_space_constraint(array, pltpu.HBM) for array in arrays]
+    specs = [HBM if pull else VMEM] * len(arrays) + [VMEM] * nstart
     out = pl.pallas_call(
         kern,
-        in_specs=[VMEM, HBM if fetch else VMEM] + [VMEM] * nstart,
+        in_specs=specs,
         out_specs=[VMEM] * len(shapes),
         out_shape=shapes,
         scratch_shapes=scratch,
         compiler_params=params(8 + duos * chunk * 256 // 1024),
         cost_estimate=cost(4 * pairs * nq * V**3, slabs.size * 2),
-    )(amps, slabs, *[s for s, _ in starts])
-    return out if give else out[0]
+    )(*arrays, *[array for pieces in starts for array, _, _ in pieces])
+    return out if pull else out[0]
 
 
 def spread_ints(ints, where):
@@ -136,8 +149,7 @@
         r, c = w_ref[0], w_ref[1]
         line = lax.broadcasted_iota(jnp.int32, (256, 32), 0) >> 4
         pair = lax.broadcasted_iota(jnp.int32, (256, 32), 1)
-        g, ii = line >> 1, line & 1
-        slot = ((g & 1) << 2) | (g & 2) | (g >> 2)
+        slot, ii = line >> 1, line & 1
         rows = jnp.where(pair == (ii << 4) + (c ^ (slot << 1)), 1.0, 0.0).astype(BF)
         picked = jnp.dot(rows, h_ref[...], preferred_element_type=F32).astype(BF)
         true = lax.broadcasted_iota(jnp.int32, (256, 512), 0)
@@ -192,34 +204,38 @@
     got_y2 = col_swap(own, 8)
     rows1 = row_swap(own, 1)
     ints = lax.dynamic_slice_in_dim(hole_ints, r * 2, 2, 0).reshape(32, 256)
+    first, where, ints = lax.optimization_barrier((own, where, ints))
     wide = spread_ints(ints, where)
-    part_0 = ladder(own, df_slabs, [], 2, fetch=True)
+    part_0, slabs = ladder([(first, 0, 2)], df_slabs, [], pull=True, chunk=16)
     near = jnp.concatenate([own, got_y2])
     got_y1 = col_swap(near, 4)
-    two_rows = jnp.concatenate([own, rows1])
+    two_rows = jnp.concatenate([first, rows1])
     rows2 = row_swap(two_rows, 4)
-    part_4 = ladder(got_y2, df_slabs, [], 2, fetch=True)
+    part_4 = ladder([(got_y2, 0, 2)], slabs, [], chunk=16)
     got_x = col_swap(jnp.concatenate([near, got_y1]), 2)
     four_rows = jnp.concatenate([two_rows, rows2])
     rows3 = row_swap(four_rows, 2)
-    part_26 = ladder(got_y1, df_slabs, [], 4, fetch=True)
+    part_26 = ladder([(got_y1, 0, 4)], slabs, [])
     mine = jnp.concatenate([four_rows, rows3])
     other = col_swap(mine, 1)
-    part_x = ladder(got_x, df_slabs, [], 8, fetch=True, chunk=16)
+    part_x = ladder([(got_x, 0, 8)], slabs, [], chunk=16)
     hole = hole_terms(wide, mine, other)
-    send_b, fetched = ladder(
-        got_x, others, [(part_x, 4), (hole, 12)], 4, 4, fetch=True, give=True, kind=BF
-    )
-    back_b = col_swap(send_b, 2).astype(F32)
-    send_a = ladder(got_x, fetched, [(part_x, 0), (hole, 8)], 4, 0, kind=BF)
-    back_a = col_swap(send_a, 2).astype(F32)
-    full_26 = ladder(got_y1, fetched, [(part_26, 0), (hole, 4)], 4)
-    back_y1 = col_swap((full_26 + back_b).astype(BF), 4).astype(F32)
-    start_04 = jnp.concatenate([part_0, part_4])
-    full_04 = ladder(near, fetched, [(start_04, 0), (hole, 0)], 4)
-    total = full_04 + back_a + back_y1
-    back_y2 = col_swap(total[2:].astype(BF), 8).astype(F32)
-    total = total[:2] + back_y2
+
+    def more(even, part, at, far, row, kind=F32, chunk=16):
+        amps = [(even, at, 2), (got_x, far, 2)]
+        starts = [[(part, at, 2), (part_x, far, 2)], [(hole, row, 4)]]
+        return ladder(amps, others, starts, kind=kind, chunk=chunk)
+
+    send_67 = more(got_y1, part_26, 2, 6, 12, BF, 8)
+    back_23 = col_swap(send_67, 8).astype(F32)
+    send_45 = more(got_y2, part_4, 0, 2, 8, BF)
+    back_01 = col_swap(send_45, 8).astype(F32)
+    full_23 = more(got_y1, part_26, 0, 4, 4)
+    near_01 = col_swap((full_23 + back_23).astype(BF), 4).astype(F32)
+    full_01 = more(first, part_0, 0, 0, 0)
+    total = full_01 + back_01 + near_01
+    last = col_swap(total[2:].astype(BF), 2).astype(F32)
+    total = total[:2] + last
     occ_first = lax.dynamic_slice_in_dim(eps_occ, r * 2, 2, 0)
     occ_second = lax.dynamic_slice_in_dim(eps_occ, c, 1, 0)
     denom = (

time: 78 us -> 66.8 us (0.86)
  the two profiles are of different devices: /device:TPU:1 before, /device:TPU:0 now
where the time goes in v2:
time: 66.8 us; the launch traced here: 66.6 us
  Pallas kernels  34.4 us (51%)
  starting transfers between devices  18.8 us (28%)
  waiting for transfers between devices  9.83 us (15%)
  local copies, waits for them, and re-layouts  1.81 us (3%)
  other arithmetic  1.6 us (2%)
    pallas_call x8, Pallas kernels, ladder(): pl.pallas_call(kern, in_specs=specs, out_specs=[VMEM] * len(shapes), out_...  32.9 us
    ppermute x9, starting transfers between devices, col_swap(): return lax.ppermute(x, 'col', [(c, c ^ mask) for c in range(16)])  10.2 us
    ppermute x3, starting transfers between devices, row_swap(): return lax.ppermute(x, 'row', [(r, r ^ mask) for r in range(8)])  8.54 us
    ppermute x3, waiting for transfers between devices, row_swap(): return lax.ppermute(x, 'row', [(r, r ^ mask) for r in range(8)])  6.12 us
    ppermute x9, waiting for transfers between devices, col_swap(): return lax.ppermute(x, 'col', [(c, c ^ mask) for c in range(16)])  3.71 us
  transfers between devices with their start and end apart: 12, of which 4 were waited for; matrix products, arithmetic and copies ran while one was open for 3% of the time, Pallas kernels for 45%

profile of v2, /device:TPU:0, one launch (start us, length us, event | category | flops | bytes accessed | tf_op | source)
XLA Modules:
  0.0 66.6 jit_solution(9679460265904869400)
XLA Ops:
  0.0 3.2 %collective-permute-start.4 = (bf16[2,128,128]{2,1,0:T(8,128)(2,1)}, bf16[2,128,128]{2,1,0:T(8,128)(2,1)S(1)}, u32[]{:S(2)}, u32[]{:S(2)}) collective-permute-start(bf16[2,128,128]{2,1,0:T(8,128)(2,1)} %bitcast.15), channel_id=1, source_target_pairs={{0,16},{16,0},{32,48},{48,32},{64,80},{80,64},{96,112},{112,96},{1... | collective-permute-start | bytes 196616 | tf_op jit(solution)/shard_map/ppermute | solution.py:23
  3.2 3.2 %collective-permute-start = (bf16[2,128,128]{2,1,0:T(8,128)(2,1)}, bf16[2,128,128]{2,1,0:T(8,128)(2,1)S(1)}, u32[]{:S(2)}, u32[]{:S(2)}) collective-permute-start(bf16[2,128,128]{2,1,0:T(8,128)(2,1)} %bitcast.16), channel_id=1, source_target_pairs={{0,8},{1,9},{2,10},{3,11},{4,12},{5,13},{6,14},{7,15},{8,0},{9,1},... | collective-permute-start | bytes 196616 | tf_op jit(solution)/shard_map/ppermute | solution.py:19
  6.7 0.9 %spread.1.w_ref = bf16[256,512]{1,0:T(8,128)(2,1)S(1)} custom-call(s32[2]{0:T(128)S(1)} %pad_add_fusion.w_ref, bf16[32,256]{1,0:T(8,128)(2,1)S(1)} %reshape.47.h_ref), custom_call_target="tpu_custom_call" | custom-call | flops 100000000 | bytes 1000000 | tf_op jit(solution)/shard_map/spread/pallas_call | solution.py:164
  7.6 0.9 %constant_dynamic-update-slice_fusion.3 = bf16[16,128,128]{2,1,0:T(8,128)(2,1)S(1)} fusion(bf16[2,128,128]{2,1,0:T(8,128)(2,1)} %bitcast.17), kind=kLoop, calls=%fused_computation.15 | loop fusion | bytes 131072
  8.5 4.0 %shard_map.64 = (f32[2,128,128]{2,1,0:T(8,128)S(1)}, bf16[64,128,128]{2,1,0:T(8,128)(2,1)S(1)}) custom-call(bf16[2,128,128]{2,1,0:T(8,128)(2,1)} %bitcast.18, bf16[64,128,128]{2,1,0:T(8,128)(2,1)} %refs_1_.1), custom_call_target="tpu_custom_call" | custom-call | flops 1073741824 | bytes 2097152 | tf_op jit(solution)/shard_map/pallas_call | solution.py:135
  12.5 4.0 %collective-permute-start.5 = (bf16[4,128,128]{2,1,0:T(8,128)(2,1)S(1)}, bf16[4,128,128]{2,1,0:T(8,128)(2,1)S(1)}, u32[]{:S(2)}, u32[]{:S(2)}) collective-permute-start(bf16[4,128,128]{2,1,0:T(8,128)(2,1)S(1)} %pad_maximum_fusion.3), channel_id=1, source_target_pairs={{0,64},{16,80},{32,96},{48,112},{64,0},{80,16},{96,32},{112,48},{1... | collective-permute-start | bytes 393224 | tf_op jit(solution)/shard_map/ppermute | solution.py:23
  16.5 0.8 %collective-permute-start.1 = (bf16[4,128,128]{2,1,0:T(8,128)(2,1)S(1)}, bf16[4,128,128]{2,1,0:T(8,128)(2,1)S(1)}, u32[]{:S(2)}, u32[]{:S(2)}) collective-permute-start(bf16[4,128,128]{2,1,0:T(8,128)(2,1)S(1)} %pad_maximum_fusion.2), channel_id=1, source_target_pairs={{0,4},{1,5},{2,6},{3,7},{4,0},{5,1},{6,2},{7,3},{8,12},{9,13},{10,... | collective-permute-start | bytes 393224 | tf_op jit(solution)/shard_map/ppermute | solution.py:19
  17.3 2.7 %collective-permute-done.5 = bf16[4,128,128]{2,1,0:T(8,128)(2,1)S(1)} collective-permute-done((bf16[4,128,128]{2,1,0:T(8,128)(2,1)S(1)}, bf16[4,128,128]{2,1,0:T(8,128)(2,1)S(1)}, u32[]{:S(2)}, u32[]{:S(2)}) %collective-permute-start.5) | collective-permute-done | bytes 131104 | tf_op jit(solution)/shard_map/ppermute | solution.py:23
  20.0 1.4 %collective-permute-start.6 = (bf16[8,128,128]{2,1,0:T(8,128)(2,1)S(1)}, bf16[8,128,128]{2,1,0:T(8,128)(2,1)S(1)}, u32[]{:S(2)}, u32[]{:S(2)}) collective-permute-start(bf16[8,128,128]{2,1,0:T(8,128)(2,1)S(1)} %pad_maximum_fusion.1), channel_id=1, source_target_pairs={{0,32},{16,48},{32,0},{48,16},{64,96},{80,112},{96,64},{112,80},{1... | collective-permute-start | bytes 786440 | tf_op jit(solution)/shard_map/ppermute | solution.py:23
  21.4 2.1 %shard_map.67.refs_3_ = f32[2,128,128]{2,1,0:T(8,128)S(1)} custom-call(bf16[2,128,128]{2,1,0:T(8,128)(2,1)S(1)} %collective-permute-done.refs_0_, bf16[64,128,128]{2,1,0:T(8,128)(2,1)S(1)} %get-tuple-element.12.refs_1_), custom_call_target="tpu_custom_call" | custom-call | flops 1073741824 | bytes 2097152 | tf_op jit(solution)/shard_map/pallas_call | solution.py:135
  23.5 0.7 %collective-permute-start.2 = (bf16[8,128,128]{2,1,0:T(8,128)(2,1)S(1)}, bf16[8,128,128]{2,1,0:T(8,128)(2,1)S(1)}, u32[]{:S(2)}, u32[]{:S(2)}) collective-permute-start(bf16[8,128,128]{2,1,0:T(8,128)(2,1)S(1)} %pad_maximum_fusion), channel_id=1, source_target_pairs={{0,2},{1,3},{2,0},{3,1},{4,6},{5,7},{6,4},{7,5},{8,10},{9,11},{10,... | collective-permute-start | bytes 786440 | tf_op jit(solution)/shard_map/ppermute | solution.py:19
  24.2 3.4 %collective-permute-done.6 = bf16[8,128,128]{2,1,0:T(8,128)(2,1)S(1)} collective-permute-done((bf16[8,128,128]{2,1,0:T(8,128)(2,1)S(1)}, bf16[8,128,128]{2,1,0:T(8,128)(2,1)S(1)}, u32[]{:S(2)}, u32[]{:S(2)}) %collective-permute-start.6) | collective-permute-done | bytes 262176 | tf_op jit(solution)/shard_map/ppermute | solution.py:23
  27.9 4.2 %shard_map.69.refs_3_ = f32[4,128,128]{2,1,0:T(8,128)S(1)} custom-call(bf16[4,128,128]{2,1,0:T(8,128)(2,1)S(1)} %collective-permute-done.1.refs_0_, bf16[64,128,128]{2,1,0:T(8,128)(2,1)S(1)} %get-tuple-element.12.refs_1_), custom_call_target="tpu_custom_call" | custom-call | flops 2147483648 | bytes 2097152 | tf_op jit(solution)/shard_map/pallas_call | solution.py:135
  32.1 6.7 %shard_map.65.refs_4_ = f32[8,128,128]{2,1,0:T(8,128)S(1)} custom-call(bf16[8,128,128]{2,1,0:T(8,128)(2,1)S(1)} %collective-permute-done.2.refs_0_.refs_1_, bf16[64,128,128]{2,1,0:T(8,128)(2,1)S(1)} %get-tuple-element.12.refs_1_), custom_call_target="tpu_custom_call" | custom-call | flops 4294967296 | bytes 2097152 | tf_op jit(solution)/shard_map/pallas_call | solution.py:135
  38.8 0.7 %hole.1.refs_5_ = f32[16,128,128]{2,1,0:T(8,128)S(1)} custom-call(bf16[256,512]{1,0:T(8,128)(2,1)S(1)} %spread.1.w_ref, bf16[16,128,128]{2,1,0:T(8,128)(2,1)S(1)} %constant_dynamic-update-slice_fusion.m_ref, bf16[16,128,128]{2,1,0:T(8,128)(2,1)S(1)} %collective-permute-done.7.p_ref), custom_call_target="tpu_custom_call" | custom-call | flops 1000000000 | bytes 1000000 | tf_op jit(solution)/shard_map/hole/pallas_call | solution.py:187
  39.6 4.2 %shard_map.71 = bf16[4,128,128]{2,1,0:T(8,128)(2,1)S(1)} custom-call(bf16[4,128,128]{2,1,0:T(8,128)(2,1)S(1)} %collective-permute-done.1.refs_0_, bf16[8,128,128]{2,1,0:T(8,128)(2,1)S(1)} %collective-permute-done.2.refs_0_.refs_1_, bf16[64,128,128]{2,1,0:T(8,128)(2,1)S(1)} %collective-permute-done.3.refs_2_, f32[4,128,128]{2,1,0:T(8,128)S(1)} %shard_map.69.refs_3_, ...), custom_call_target="tpu_custom_call" | custom-call | flops 2147483648 | bytes 2097152 | tf_op jit(solution)/shard_map/pallas_call | solution.py:135
  44.4 3.9 %shard_map.68 = bf16[4,128,128]{2,1,0:T(8,128)(2,1)S(1)} custom-call(bf16[2,128,128]{2,1,0:T(8,128)(2,1)S(1)} %collective-permute-done.refs_0_, bf16[8,128,128]{2,1,0:T(8,128)(2,1)S(1)} %collective-permute-done.2.refs_0_.refs_1_, bf16[64,128,128]{2,1,0:T(8,128)(2,1)S(1)} %collective-permute-done.3.refs_2_, f32[2,128,128]{2,1,0:T(8,128)S(1)} %shard_map.67.refs_3_, ...), custom_call_target="tpu_custom_call" | custom-call | flops 2147483648 | bytes 2097152 | tf_op jit(solution)/shard_map/pallas_call | solution.py:135
  48.3 3.3 %collective-permute-start.8 = (bf16[4,128,128]{2,1,0:T(8,128)(2,1)S(1)}, bf16[4,128,128]{2,1,0:T(8,128)(2,1)S(1)}, u32[]{:S(2)}, u32[]{:S(2)}) collective-permute-start(bf16[4,128,128]{2,1,0:T(8,128)(2,1)S(1)} %shard_map.68), channel_id=1, source_target_pairs={{0,8},{1,9},{2,10},{3,11},{4,12},{5,13},{6,14},{7,15},{8,0},{9,1},... | collective-permute-start | bytes 393224 | tf_op jit(solution)/shard_map/ppermute | solution.py:19
  51.6 3.9 %shard_map.70 = f32[4,128,128]{2,1,0:T(8,128)S(1)} custom-call(bf16[4,128,128]{2,1,0:T(8,128)(2,1)S(1)} %collective-permute-done.1.refs_0_, bf16[8,128,128]{2,1,0:T(8,128)(2,1)S(1)} %collective-permute-done.2.refs_0_.refs_1_, bf16[64,128,128]{2,1,0:T(8,128)(2,1)S(1)} %collective-permute-done.3.refs_2_, f32[4,128,128]{2,1,0:T(8,128)S(1)} %shard_map.69.refs_3_, ...), custom_call_target="tpu_custom_call" | custom-call | flops 2147483648 | bytes 2097152 | tf_op jit(solution)/shard_map/pallas_call | solution.py:135
  55.5 0.8 %collective-permute-start.10 = (bf16[4,128,128]{2,1,0:T(8,128)(2,1)S(1)}, bf16[4,128,128]{2,1,0:T(8,128)(2,1)S(1)}, u32[]{:S(2)}, u32[]{:S(2)}) collective-permute-start(bf16[4,128,128]{2,1,0:T(8,128)(2,1)S(1)} %add_convert_fusion), channel_id=1, source_target_pairs={{0,4},{1,5},{2,6},{3,7},{4,0},{5,1},{6,2},{7,3},{8,12},{9,13},{10,... | collective-permute-start | bytes 393224 | tf_op jit(solution)/shard_map/ppermute | solution.py:19
  56.3 3.9 %shard_map.66 = f32[4,128,128]{2,1,0:T(8,128)S(1)} custom-call(bf16[2,128,128]{2,1,0:T(8,128)(2,1)S(1)} %bitcast.23, bf16[8,128,128]{2,1,0:T(8,128)(2,1)S(1)} %collective-permute-done.2.refs_0_.refs_1_, bf16[64,128,128]{2,1,0:T(8,128)(2,1)S(1)} %collective-permute-done.3.refs_2_, f32[2,128,128]{2,1,0:T(8,128)S(1)} %get-tuple-element.11.refs_3_, ...), custom_call_target="tpu_custom_call" | custom-call | flops 2147483648 | bytes 2097152 | tf_op jit(solution)/shard_map/pallas_call | solution.py:135
  60.2 0.7 %collective-permute-done.10 = bf16[4,128,128]{2,1,0:T(8,128)(2,1)S(1)} collective-permute-done((bf16[4,128,128]{2,1,0:T(8,128)(2,1)S(1)}, bf16[4,128,128]{2,1,0:T(8,128)(2,1)S(1)}, u32[]{:S(2)}, u32[]{:S(2)}) %collective-permute-start.10) | collective-permute-done | bytes 131104 | tf_op jit(solution)/shard_map/ppermute | solution.py:19
  62.4 3.0 %collective-permute-done.11 = bf16[2,128,128]{2,1,0:T(8,128)(2,1)S(1)} collective-permute-done((bf16[2,128,128]{2,1,0:T(8,128)(2,1)S(1)}, bf16[2,128,128]{2,1,0:T(8,128)(2,1)S(1)}, u32[]{:S(2)}, u32[]{:S(2)}) %collective-permute-start.11) | collective-permute-done | bytes 65568 | tf_op jit(solution)/shard_map/ppermute | solution.py:19
  65.3 1.3 %fusion.2 = f32[2,1,128,128]{3,2,1,0:T(8,128)} fusion(f32[4,128,128]{2,1,0:T(8,128)S(1)} %convert_add_fusion, bf16[2,128,128]{2,1,0:T(8,128)(2,1)S(1)} %collective-permute-done.11, bf16[2,1,128,128]{3,2,1,0:T(8,128)(2,1)S(1)} %copy-done.2, f32[]{:T(128)} %bitcast.5, f32[2]{0:T(128)S(1)} %dynamic_slice.10, f32[128,128]{1,0:T(8,128)S(1)} %broadcast_add_fusion), kind=kLoop, calls=%fused_computation.8 | loop fusion | flops 229376 | bytes 458764 | tf_op jit(solution)/shard_map/reshape | solution.py:247
  (38 shorter events, 2.8 us)
Async XLA Ops:
  0.0 6.4 %copy-start = (bf16[16,16,16,16]{3,2,1,0:T(8,128)(2,1)S(1)}, bf16[16,16,16,16]{3,2,1,0:T(8,128)(2,1)}, u32[]{:S(2)}) copy-start(bf16[16,16,16,16]{3,2,1,0:T(8,128)(2,1)} %param.9) | copy-start | bytes 393220
  0.0 39.5 %collective-permute-start.3 = (bf16[64,128,128]{2,1,0:T(8,128)(2,1)}, bf16[64,128,128]{2,1,0:T(8,128)(2,1)S(1)}, u32[]{:S(2)}, u32[]{:S(2)}) collective-permute-start(bf16[64,128,128]{2,1,0:T(8,128)(2,1)} %refs_1_.1), channel_id=1, source_target_pairs={{0,1},{1,0},{2,3},{3,2},{4,5},{5,4},{6,7},{7,6},{8,9},{9,8},{10,11... | collective-permute-start | bytes 6291464 | tf_op jit(solution)/shard_map/ppermute | solution.py:19
  0.0 12.5 %collective-permute-start.4 = (bf16[2,128,128]{2,1,0:T(8,128)(2,1)}, bf16[2,128,128]{2,1,0:T(8,128)(2,1)S(1)}, u32[]{:S(2)}, u32[]{:S(2)}) collective-permute-start(bf16[2,128,128]{2,1,0:T(8,128)(2,1)} %bitcast.15), channel_id=1, source_target_pairs={{0,16},{16,0},{32,48},{48,32},{64,80},{80,64},{96,112},{112,96},{1... | collective-permute-start | bytes 196616 | tf_op jit(solution)/shard_map/ppermute | solution.py:23
  3.2 13.2 %collective-permute-start = (bf16[2,128,128]{2,1,0:T(8,128)(2,1)}, bf16[2,128,128]{2,1,0:T(8,128)(2,1)S(1)}, u32[]{:S(2)}, u32[]{:S(2)}) collective-permute-start(bf16[2,128,128]{2,1,0:T(8,128)(2,1)} %bitcast.16), channel_id=1, source_target_pairs={{0,8},{1,9},{2,10},{3,11},{4,12},{5,13},{6,14},{7,15},{8,0},{9,1},... | collective-permute-start | bytes 196616 | tf_op jit(solution)/shard_map/ppermute | solution.py:19
  7.5 4.9 %copy-start.1 = (bf16[2,1,128,128]{3,2,1,0:T(8,128)(2,1)S(1)}, bf16[2,1,128,128]{3,2,1,0:T(8,128)(2,1)}, u32[]{:S(2)}) copy-start(bf16[2,1,128,128]{3,2,1,0:T(8,128)(2,1)} %param.6) | copy-start | bytes 196612
  12.5 7.5 %collective-permute-start.5 = (bf16[4,128,128]{2,1,0:T(8,128)(2,1)S(1)}, bf16[4,128,128]{2,1,0:T(8,128)(2,1)S(1)}, u32[]{:S(2)}, u32[]{:S(2)}) collective-permute-start(bf16[4,128,128]{2,1,0:T(8,128)(2,1)S(1)} %pad_maximum_fusion.3), channel_id=1, source_target_pairs={{0,64},{16,80},{32,96},{48,112},{64,0},{80,16},{96,32},{112,48},{1... | collective-permute-start | bytes 393224 | tf_op jit(solution)/shard_map/ppermute | solution.py:23
  16.5 7.0 %collective-permute-start.1 = (bf16[4,128,128]{2,1,0:T(8,128)(2,1)S(1)}, bf16[4,128,128]{2,1,0:T(8,128)(2,1)S(1)}, u32[]{:S(2)}, u32[]{:S(2)}) collective-permute-start(bf16[4,128,128]{2,1,0:T(8,128)(2,1)S(1)} %pad_maximum_fusion.2), channel_id=1, source_target_pairs={{0,4},{1,5},{2,6},{3,7},{4,0},{5,1},{6,2},{7,3},{8,12},{9,13},{10,... | collective-permute-start | bytes 393224 | tf_op jit(solution)/shard_map/ppermute | solution.py:19
  20.0 7.6 %collective-permute-start.6 = (bf16[8,128,128]{2,1,0:T(8,128)(2,1)S(1)}, bf16[8,128,128]{2,1,0:T(8,128)(2,1)S(1)}, u32[]{:S(2)}, u32[]{:S(2)}) collective-permute-start(bf16[8,128,128]{2,1,0:T(8,128)(2,1)S(1)} %pad_maximum_fusion.1), channel_id=1, source_target_pairs={{0,32},{16,48},{32,0},{48,16},{64,96},{80,112},{96,64},{112,80},{1... | collective-permute-start | bytes 786440 | tf_op jit(solution)/shard_map/ppermute | solution.py:23
  23.5 8.6 %collective-permute-start.2 = (bf16[8,128,128]{2,1,0:T(8,128)(2,1)S(1)}, bf16[8,128,128]{2,1,0:T(8,128)(2,1)S(1)}, u32[]{:S(2)}, u32[]{:S(2)}) collective-permute-start(bf16[8,128,128]{2,1,0:T(8,128)(2,1)S(1)} %pad_maximum_fusion), channel_id=1, source_target_pairs={{0,2},{1,3},{2,0},{3,1},{4,6},{5,7},{6,4},{7,5},{8,10},{9,11},{10,... | collective-permute-start | bytes 786440 | tf_op jit(solution)/shard_map/ppermute | solution.py:19
  27.6 11.2 %collective-permute-start.7 = (bf16[16,128,128]{2,1,0:T(8,128)(2,1)S(1)}, bf16[16,128,128]{2,1,0:T(8,128)(2,1)S(1)}, u32[]{:S(2)}, u32[]{:S(2)}) collective-permute-start(bf16[16,128,128]{2,1,0:T(8,128)(2,1)S(1)} %constant_dynamic-update-slice_fusion.m_ref), channel_id=1, source_target_pairs={{0,1},{1,0},{2,3},{3,2},{4,5},{5,4},{6,7},{7,6},{8,9},{9,8},{10,11... | collective-permute-start | bytes 1572872 | tf_op jit(solution)/shard_map/ppermute | solution.py:19
  43.8 11.7 %collective-permute-start.9 = (bf16[4,128,128]{2,1,0:T(8,128)(2,1)S(1)}, bf16[4,128,128]{2,1,0:T(8,128)(2,1)S(1)}, u32[]{:S(2)}, u32[]{:S(2)}) collective-permute-start(bf16[4,128,128]{2,1,0:T(8,128)(2,1)S(1)} %shard_map.71), channel_id=1, source_target_pairs={{0,8},{1,9},{2,10},{3,11},{4,12},{5,13},{6,14},{7,15},{8,0},{9,1},... | collective-permute-start | bytes 393224 | tf_op jit(solution)/shard_map/ppermute | solution.py:19
  48.3 11.9 %collective-permute-start.8 = (bf16[4,128,128]{2,1,0:T(8,128)(2,1)S(1)}, bf16[4,128,128]{2,1,0:T(8,128)(2,1)S(1)}, u32[]{:S(2)}, u32[]{:S(2)}) collective-permute-start(bf16[4,128,128]{2,1,0:T(8,128)(2,1)S(1)} %shard_map.68), channel_id=1, source_target_pairs={{0,8},{1,9},{2,10},{3,11},{4,12},{5,13},{6,14},{7,15},{8,0},{9,1},... | collective-permute-start | bytes 393224 | tf_op jit(solution)/shard_map/ppermute | solution.py:19
  55.5 5.4 %collective-permute-start.10 = (bf16[4,128,128]{2,1,0:T(8,128)(2,1)S(1)}, bf16[4,128,128]{2,1,0:T(8,128)(2,1)S(1)}, u32[]{:S(2)}, u32[]{:S(2)}) collective-permute-start(bf16[4,128,128]{2,1,0:T(8,128)(2,1)S(1)} %add_convert_fusion), channel_id=1, source_target_pairs={{0,4},{1,5},{2,6},{3,7},{4,0},{5,1},{6,2},{7,3},{8,12},{9,13},{10,... | collective-permute-start | bytes 393224 | tf_op jit(solution)/shard_map/ppermute | solution.py:19
  56.3 5.4 %copy-start.3 = (f32[128]{0:T(128)S(1)}, f32[128]{0:T(128)}, u32[]{:S(2)}) copy-start(f32[128]{0:T(128)} %param.11) | copy-start | bytes 1540
  56.3 5.5 %copy-start.4 = (f32[16]{0:T(128)S(1)}, f32[16]{0:T(128)}, u32[]{:S(2)}) copy-start(f32[16]{0:T(128)} %param.10) | copy-start | bytes 196
  56.3 9.1 %copy-start.2 = (bf16[2,1,128,128]{3,2,1,0:T(8,128)(2,1)S(1)}, bf16[2,1,128,128]{3,2,1,0:T(8,128)(2,1)}, u32[]{:S(2)}) copy-start(bf16[2,1,128,128]{3,2,1,0:T(8,128)(2,1)} %param.8) | copy-start | bytes 196612
  61.0 4.3 %collective-permute-start.11 = (bf16[2,128,128]{2,1,0:T(8,128)(2,1)S(1)}, bf16[2,128,128]{2,1,0:T(8,128)(2,1)S(1)}, u32[]{:S(2)}, u32[]{:S(2)}) collective-permute-start(bf16[2,128,128]{2,1,0:T(8,128)(2,1)S(1)} %slice.19), channel_id=1, source_target_pairs={{0,2},{1,3},{2,0},{3,1},{4,6},{5,7},{6,4},{7,5},{8,10},{9,11},{10,... | collective-permute-start | bytes 196616 | tf_op jit(solution)/shard_map/ppermute | solution.py:19

commit v3 on v2

--- a/solution.py
+++ b/solution.py
@@ -172,8 +172,8 @@
     )(where, ints)
 
 
-def hole_terms(wide, mine, other):
-    def kern(w_ref, m_ref, p_ref, o_ref):
+def hole_terms(wide, mine, other, ahead):
+    def kern(w_ref, m_ref, p_ref, a_ref, s_ref, o_ref):
         for ga in range(8):
             rows = slice(ga * 16, (ga + 1) * 16)
             stack = jnp.concatenate(
@@ -181,18 +181,24 @@
                 axis=0,
             )
             terms = jnp.dot(w_ref[...], stack, preferred_element_type=F32)
-            for n in range(16):
+            for n in range(12):
                 o_ref[n, rows, :] = terms[n * 16 : (n + 1) * 16]
+            for n in range(4):
+                value = terms[(12 + n) * 16 : (13 + n) * 16]
+                s_ref[n, rows, :] = (a_ref[n, rows, :] + value).astype(BF)
 
     return pl.pallas_call(
         kern,
-        in_specs=[VMEM] * 3,
-        out_specs=VMEM,
-        out_shape=jax.ShapeDtypeStruct((16, V, V), F32),
+        in_specs=[VMEM] * 4,
+        out_specs=[VMEM] * 2,
+        out_shape=[
+            jax.ShapeDtypeStruct((4, V, V), BF),
+            jax.ShapeDtypeStruct((12, V, V), F32),
+        ],
         compiler_params=params(8),
         cost_estimate=cost(10**9, 10**6),
         name="hole",
-    )(wide, mine, other)
+    )(wide, mine, other, ahead)
 
 
 def body(t_amps, df_slabs, drive, hole_ints, eps_occ, eps_vir):
@@ -215,24 +221,24 @@
     got_x = col_swap(jnp.concatenate([near, got_y1]), 2)
     four_rows = jnp.concatenate([two_rows, rows2])
     rows3 = row_swap(four_rows, 2)
-    part_26 = ladder([(got_y1, 0, 4)], slabs, [])
+    part_26 = ladder([(got_y1, 0, 4)], slabs, [], chunk=16)
     mine = jnp.concatenate([four_rows, rows3])
     other = col_swap(mine, 1)
     part_x = ladder([(got_x, 0, 8)], slabs, [], chunk=16)
-    hole = hole_terms(wide, mine, other)
-
-    def more(even, part, at, far, row, kind=F32, chunk=16):
+
+    def more(even, part, at, far, extra=(), kind=F32):
         amps = [(even, at, 2), (got_x, far, 2)]
-        starts = [[(part, at, 2), (part_x, far, 2)], [(hole, row, 4)]]
-        return ladder(amps, others, starts, kind=kind, chunk=chunk)
-
-    send_67 = more(got_y1, part_26, 2, 6, 12, BF, 8)
+        starts = [[(part, at, 2), (part_x, far, 2)]] + [[piece] for piece in extra]
+        return ladder(amps, others, starts, kind=kind, chunk=16)
+
+    full_67 = more(got_y1, part_26, 2, 6)
+    send_67, hole = hole_terms(wide, mine, other, full_67)
     back_23 = col_swap(send_67, 8).astype(F32)
-    send_45 = more(got_y2, part_4, 0, 2, 8, BF)
+    send_45 = more(got_y2, part_4, 0, 2, [(hole, 8, 4)], BF)
     back_01 = col_swap(send_45, 8).astype(F32)
-    full_23 = more(got_y1, part_26, 0, 4, 4)
+    full_23 = more(got_y1, part_26, 0, 4, [(hole, 4, 4)])
     near_01 = col_swap((full_23 + back_23).astype(BF), 4).astype(F32)
-    full_01 = more(first, part_0, 0, 0, 0)
+    full_01 = more(first, part_0, 0, 0, [(hole, 0, 4)])
     total = full_01 + back_01 + near_01
     last = col_swap(total[2:].astype(BF), 2).astype(F32)
     total = total[:2] + last

time: 66.8 us -> 62.7 us (0.939)
  the two profiles are of different devices: /device:TPU:0 before, /device:TPU:1 now
where the time goes in v3:
time: 62.7 us; the launch traced here: 61.8 us
  Pallas kernels  33.8 us (54%)
  starting transfers between devices  20.5 us (33%)
  waiting for transfers between devices  3.65 us (6%)
  local copies, waits for them, and re-layouts  1.92 us (3%)
  other arithmetic  1.75 us (3%)
    pallas_call x8, Pallas kernels, ladder(): pl.pallas_call(kern, in_specs=specs, out_specs=[VMEM] * len(shapes), out_...  32.3 us
    ppermute x9, starting transfers between devices, col_swap(): return lax.ppermute(x, 'col', [(c, c ^ mask) for c in range(16)])  13.1 us
    ppermute x3, starting transfers between devices, row_swap(): return lax.ppermute(x, 'row', [(r, r ^ mask) for r in range(8)])  7.34 us
    ppermute x3, waiting for transfers between devices, row_swap(): return lax.ppermute(x, 'row', [(r, r ^ mask) for r in range(8)])  2.11 us
    ppermute x9, waiting for transfers between devices, col_swap(): return lax.ppermute(x, 'col', [(c, c ^ mask) for c in range(16)])  1.54 us
    reshape x1, other arithmetic, body(): ((drive.reshape(2, V, V).astype(F32) + total) / denom).reshape(2, 1, V, V)  1.43 us
  transfers between devices with their start and end apart: 12, of which 3 were waited for; matrix products, arithmetic and copies ran while one was open for 3% of the time, Pallas kernels for 54%

profile of v3, /device:TPU:1, one launch (start us, length us, event | category | flops | bytes accessed | tf_op | source)
XLA Modules:
  0.0 61.8 jit_solution(6701957522656111443)
XLA Ops:
  0.0 1.4 %collective-permute-start.3 = (bf16[64,128,128]{2,1,0:T(8,128)(2,1)}, bf16[64,128,128]{2,1,0:T(8,128)(2,1)S(1)}, u32[]{:S(2)}, u32[]{:S(2)}) collective-permute-start(bf16[64,128,128]{2,1,0:T(8,128)(2,1)} %refs_1_.1), channel_id=1, source_target_pairs={{0,1},{1,0},{2,3},{3,2},{4,5},{5,4},{6,7},{7,6},{8,9},{9,8},{10,11... | collective-permute-start | bytes 6291464 | tf_op jit(solution)/shard_map/ppermute | solution.py:19
  1.4 2.9 %collective-permute-start.4 = (bf16[2,128,128]{2,1,0:T(8,128)(2,1)}, bf16[2,128,128]{2,1,0:T(8,128)(2,1)S(1)}, u32[]{:S(2)}, u32[]{:S(2)}) collective-permute-start(bf16[2,128,128]{2,1,0:T(8,128)(2,1)} %bitcast.15), channel_id=1, source_target_pairs={{0,16},{16,0},{32,48},{48,32},{64,80},{80,64},{96,112},{112,96},{1... | collective-permute-start | bytes 196616 | tf_op jit(solution)/shard_map/ppermute | solution.py:23
  4.2 2.9 %collective-permute-start = (bf16[2,128,128]{2,1,0:T(8,128)(2,1)}, bf16[2,128,128]{2,1,0:T(8,128)(2,1)S(1)}, u32[]{:S(2)}, u32[]{:S(2)}) collective-permute-start(bf16[2,128,128]{2,1,0:T(8,128)(2,1)} %bitcast.16), channel_id=1, source_target_pairs={{0,8},{1,9},{2,10},{3,11},{4,12},{5,13},{6,14},{7,15},{8,0},{9,1},... | collective-permute-start | bytes 196616 | tf_op jit(solution)/shard_map/ppermute | solution.py:19
  7.4 0.9 %spread.1.w_ref = bf16[256,512]{1,0:T(8,128)(2,1)S(1)} custom-call(s32[2]{0:T(128)S(1)} %pad_add_fusion.w_ref, bf16[32,256]{1,0:T(8,128)(2,1)S(1)} %reshape.47.h_ref), custom_call_target="tpu_custom_call" | custom-call | flops 100000000 | bytes 1000000 | tf_op jit(solution)/shard_map/spread/pallas_call | solution.py:164
  8.3 0.9 %constant_dynamic-update-slice_fusion.3 = bf16[16,128,128]{2,1,0:T(8,128)(2,1)S(1)} fusion(bf16[2,128,128]{2,1,0:T(8,128)(2,1)} %bitcast.17), kind=kLoop, calls=%fused_computation.15 | loop fusion | bytes 131072
  9.2 4.0 %shard_map.64 = (f32[2,128,128]{2,1,0:T(8,128)S(1)}, bf16[64,128,128]{2,1,0:T(8,128)(2,1)S(1)}) custom-call(bf16[2,128,128]{2,1,0:T(8,128)(2,1)} %bitcast.18, bf16[64,128,128]{2,1,0:T(8,128)(2,1)} %refs_1_.1), custom_call_target="tpu_custom_call" | custom-call | flops 1073741824 | bytes 2097152 | tf_op jit(solution)/shard_map/pallas_call | solution.py:135
  13.7 3.7 %collective-permute-start.5 = (bf16[4,128,128]{2,1,0:T(8,128)(2,1)S(1)}, bf16[4,128,128]{2,1,0:T(8,128)(2,1)S(1)}, u32[]{:S(2)}, u32[]{:S(2)}) collective-permute-start(bf16[4,128,128]{2,1,0:T(8,128)(2,1)S(1)} %pad_maximum_fusion.3), channel_id=1, source_target_pairs={{0,64},{16,80},{32,96},{48,112},{64,0},{80,16},{96,32},{112,48},{1... | collective-permute-start | bytes 393224 | tf_op jit(solution)/shard_map/ppermute | solution.py:23
  17.4 2.1 %shard_map.69.refs_3_ = f32[2,128,128]{2,1,0:T(8,128)S(1)} custom-call(bf16[2,128,128]{2,1,0:T(8,128)(2,1)S(1)} %collective-permute-done.refs_0_, bf16[64,128,128]{2,1,0:T(8,128)(2,1)S(1)} %get-tuple-element.14.refs_1_), custom_call_target="tpu_custom_call" | custom-call | flops 1073741824 | bytes 2097152 | tf_op jit(solution)/shard_map/pallas_call | solution.py:135
  20.4 0.8 %collective-permute-start.6 = (bf16[8,128,128]{2,1,0:T(8,128)(2,1)S(1)}, bf16[8,128,128]{2,1,0:T(8,128)(2,1)S(1)}, u32[]{:S(2)}, u32[]{:S(2)}) collective-permute-start(bf16[8,128,128]{2,1,0:T(8,128)(2,1)S(1)} %pad_maximum_fusion.1), channel_id=1, source_target_pairs={{0,32},{16,48},{32,0},{48,16},{64,96},{80,112},{96,64},{112,80},{1... | collective-permute-start | bytes 786440 | tf_op jit(solution)/shard_map/ppermute | solution.py:23
  21.2 3.9 %shard_map.66.refs_3_ = f32[4,128,128]{2,1,0:T(8,128)S(1)} custom-call(bf16[4,128,128]{2,1,0:T(8,128)(2,1)S(1)} %collective-permute-done.1.refs_0_, bf16[64,128,128]{2,1,0:T(8,128)(2,1)S(1)} %get-tuple-element.14.refs_1_), custom_call_target="tpu_custom_call" | custom-call | flops 2147483648 | bytes 2097152 | tf_op jit(solution)/shard_map/pallas_call | solution.py:135
  25.1 1.7 %collective-permute-done.6 = bf16[8,128,128]{2,1,0:T(8,128)(2,1)S(1)} collective-permute-done((bf16[8,128,128]{2,1,0:T(8,128)(2,1)S(1)}, bf16[8,128,128]{2,1,0:T(8,128)(2,1)S(1)}, u32[]{:S(2)}, u32[]{:S(2)}) %collective-permute-start.6) | collective-permute-done | bytes 262176 | tf_op jit(solution)/shard_map/ppermute | solution.py:23
  26.9 2.6 %collective-permute-start.7 = (bf16[16,128,128]{2,1,0:T(8,128)(2,1)S(1)}, bf16[16,128,128]{2,1,0:T(8,128)(2,1)S(1)}, u32[]{:S(2)}, u32[]{:S(2)}) collective-permute-start(bf16[16,128,128]{2,1,0:T(8,128)(2,1)S(1)} %constant_dynamic-update-slice_fusion.m_ref), channel_id=1, source_target_pairs={{0,1},{1,0},{2,3},{3,2},{4,5},{5,4},{6,7},{7,6},{8,9},{9,8},{10,11... | collective-permute-start | bytes 1572872 | tf_op jit(solution)/shard_map/ppermute | solution.py:19
  29.5 6.7 %shard_map.65.refs_4_ = f32[8,128,128]{2,1,0:T(8,128)S(1)} custom-call(bf16[8,128,128]{2,1,0:T(8,128)(2,1)S(1)} %collective-permute-done.2.refs_0_.refs_1_, bf16[64,128,128]{2,1,0:T(8,128)(2,1)S(1)} %get-tuple-element.14.refs_1_), custom_call_target="tpu_custom_call" | custom-call | flops 4294967296 | bytes 2097152 | tf_op jit(solution)/shard_map/pallas_call | solution.py:135
  36.2 3.9 %shard_map.67.a_ref = f32[4,128,128]{2,1,0:T(8,128)S(1)} custom-call(bf16[4,128,128]{2,1,0:T(8,128)(2,1)S(1)} %collective-permute-done.1.refs_0_, bf16[8,128,128]{2,1,0:T(8,128)(2,1)S(1)} %collective-permute-done.2.refs_0_.refs_1_, bf16[64,128,128]{2,1,0:T(8,128)(2,1)S(1)} %collective-permute-done.3.refs_2_, f32[4,128,128]{2,1,0:T(8,128)S(1)} %shard_map.66.refs_3_, ...), custom_call_target="tpu_custom_call" | custom-call | flops 2147483648 | bytes 2097152 | tf_op jit(solution)/shard_map/pallas_call | solution.py:135
  40.1 0.7 %hole.1 = (bf16[4,128,128]{2,1,0:T(8,128)(2,1)S(1)}, f32[12,128,128]{2,1,0:T(8,128)S(1)}) custom-call(bf16[256,512]{1,0:T(8,128)(2,1)S(1)} %spread.1.w_ref, bf16[16,128,128]{2,1,0:T(8,128)(2,1)S(1)} %constant_dynamic-update-slice_fusion.m_ref, bf16[16,128,128]{2,1,0:T(8,128)(2,1)S(1)} %collective-permute-done.7.p_ref, f32[4,128,128]{2,1,0:T(8,128)S(1)} %shard_map.67.a_ref), custom_call_target="tpu_custom_call" | custom-call | flops 1000000000 | bytes 1000000 | tf_op jit(solution)/shard_map/hole/pallas_call | solution.py:190
  40.8 1.9 %collective-permute-start.9 = (bf16[4,128,128]{2,1,0:T(8,128)(2,1)S(1)}, bf16[4,128,128]{2,1,0:T(8,128)(2,1)S(1)}, u32[]{:S(2)}, u32[]{:S(2)}) collective-permute-start(bf16[4,128,128]{2,1,0:T(8,128)(2,1)S(1)} %get-tuple-element.18), channel_id=1, source_target_pairs={{0,8},{1,9},{2,10},{3,11},{4,12},{5,13},{6,14},{7,15},{8,0},{9,1},... | collective-permute-start | bytes 393224 | tf_op jit(solution)/shard_map/ppermute | solution.py:19
  42.7 3.9 %shard_map.70 = bf16[4,128,128]{2,1,0:T(8,128)(2,1)S(1)} custom-call(bf16[2,128,128]{2,1,0:T(8,128)(2,1)S(1)} %collective-permute-done.refs_0_, bf16[8,128,128]{2,1,0:T(8,128)(2,1)S(1)} %collective-permute-done.2.refs_0_.refs_1_, bf16[64,128,128]{2,1,0:T(8,128)(2,1)S(1)} %collective-permute-done.3.refs_2_, f32[2,128,128]{2,1,0:T(8,128)S(1)} %shard_map.69.refs_3_, ...), custom_call_target="tpu_custom_call" | custom-call | flops 2147483648 | bytes 2097152 | tf_op jit(solution)/shard_map/pallas_call | solution.py:135
  46.6 1.5 %collective-permute-start.8 = (bf16[4,128,128]{2,1,0:T(8,128)(2,1)S(1)}, bf16[4,128,128]{2,1,0:T(8,128)(2,1)S(1)}, u32[]{:S(2)}, u32[]{:S(2)}) collective-permute-start(bf16[4,128,128]{2,1,0:T(8,128)(2,1)S(1)} %shard_map.70), channel_id=1, source_target_pairs={{0,8},{1,9},{2,10},{3,11},{4,12},{5,13},{6,14},{7,15},{8,0},{9,1},... | collective-permute-start | bytes 393224 | tf_op jit(solution)/shard_map/ppermute | solution.py:19
  48.1 3.9 %shard_map.71 = f32[4,128,128]{2,1,0:T(8,128)S(1)} custom-call(bf16[4,128,128]{2,1,0:T(8,128)(2,1)S(1)} %collective-permute-done.1.refs_0_, bf16[8,128,128]{2,1,0:T(8,128)(2,1)S(1)} %collective-permute-done.2.refs_0_.refs_1_, bf16[64,128,128]{2,1,0:T(8,128)(2,1)S(1)} %collective-permute-done.3.refs_2_, f32[4,128,128]{2,1,0:T(8,128)S(1)} %shard_map.66.refs_3_, ...), custom_call_target="tpu_custom_call" | custom-call | flops 2147483648 | bytes 2097152 | tf_op jit(solution)/shard_map/pallas_call | solution.py:135
  52.1 1.1 %collective-permute-start.10 = (bf16[4,128,128]{2,1,0:T(8,128)(2,1)S(1)}, bf16[4,128,128]{2,1,0:T(8,128)(2,1)S(1)}, u32[]{:S(2)}, u32[]{:S(2)}) collective-permute-start(bf16[4,128,128]{2,1,0:T(8,128)(2,1)S(1)} %add_convert_fusion), channel_id=1, source_target_pairs={{0,4},{1,5},{2,6},{3,7},{4,0},{5,1},{6,2},{7,3},{8,12},{9,13},{10,... | collective-permute-start | bytes 393224 | tf_op jit(solution)/shard_map/ppermute | solution.py:19
  53.2 3.9 %shard_map.68 = f32[4,128,128]{2,1,0:T(8,128)S(1)} custom-call(bf16[2,128,128]{2,1,0:T(8,128)(2,1)S(1)} %bitcast.23, bf16[8,128,128]{2,1,0:T(8,128)(2,1)S(1)} %collective-permute-done.2.refs_0_.refs_1_, bf16[64,128,128]{2,1,0:T(8,128)(2,1)S(1)} %collective-permute-done.3.refs_2_, f32[2,128,128]{2,1,0:T(8,128)S(1)} %get-tuple-element.13.refs_3_, ...), custom_call_target="tpu_custom_call" | custom-call | flops 2147483648 | bytes 2097152 | tf_op jit(solution)/shard_map/pallas_call | solution.py:135
  57.2 0.8 %collective-permute-start.11 = (bf16[2,128,128]{2,1,0:T(8,128)(2,1)S(1)}, bf16[2,128,128]{2,1,0:T(8,128)(2,1)S(1)}, u32[]{:S(2)}, u32[]{:S(2)}) collective-permute-start(bf16[2,128,128]{2,1,0:T(8,128)(2,1)S(1)} %slice.19), channel_id=1, source_target_pairs={{0,2},{1,3},{2,0},{3,1},{4,6},{5,7},{6,4},{7,5},{8,10},{9,11},{10,... | collective-permute-start | bytes 196616 | tf_op jit(solution)/shard_map/ppermute | solution.py:19
  58.9 1.5 %collective-permute-done.11 = bf16[2,128,128]{2,1,0:T(8,128)(2,1)S(1)} collective-permute-done((bf16[2,128,128]{2,1,0:T(8,128)(2,1)S(1)}, bf16[2,128,128]{2,1,0:T(8,128)(2,1)S(1)}, u32[]{:S(2)}, u32[]{:S(2)}) %collective-permute-start.11) | collective-permute-done | bytes 65568 | tf_op jit(solution)/shard_map/ppermute | solution.py:19
  60.4 1.4 %fusion.2 = f32[2,1,128,128]{3,2,1,0:T(8,128)} fusion(f32[4,128,128]{2,1,0:T(8,128)S(1)} %convert_add_fusion, bf16[2,128,128]{2,1,0:T(8,128)(2,1)S(1)} %collective-permute-done.11, bf16[2,1,128,128]{3,2,1,0:T(8,128)(2,1)S(1)} %copy-done.2, f32[]{:T(128)} %bitcast.5, f32[2]{0:T(128)S(1)} %dynamic_slice.10, f32[128,128]{1,0:T(8,128)S(1)} %broadcast_add_fusion), kind=kLoop, calls=%fused_computation.8 | loop fusion | flops 229376 | bytes 458764 | tf_op jit(solution)/shard_map/reshape | solution.py:253
  (38 shorter events, 2.6 us)
Async XLA Ops:
  0.0 7.2 %copy-start = (bf16[16,16,16,16]{3,2,1,0:T(8,128)(2,1)S(1)}, bf16[16,16,16,16]{3,2,1,0:T(8,128)(2,1)}, u32[]{:S(2)}) copy-start(bf16[16,16,16,16]{3,2,1,0:T(8,128)(2,1)} %param.9) | copy-start | bytes 393220
  0.0 36.2 %collective-permute-start.3 = (bf16[64,128,128]{2,1,0:T(8,128)(2,1)}, bf16[64,128,128]{2,1,0:T(8,128)(2,1)S(1)}, u32[]{:S(2)}, u32[]{:S(2)}) collective-permute-start(bf16[64,128,128]{2,1,0:T(8,128)(2,1)} %refs_1_.1), channel_id=1, source_target_pairs={{0,1},{1,0},{2,3},{3,2},{4,5},{5,4},{6,7},{7,6},{8,9},{9,8},{10,11... | collective-permute-start | bytes 6291464 | tf_op jit(solution)/shard_map/ppermute | solution.py:19
  1.4 12.3 %collective-permute-start.4 = (bf16[2,128,128]{2,1,0:T(8,128)(2,1)}, bf16[2,128,128]{2,1,0:T(8,128)(2,1)S(1)}, u32[]{:S(2)}, u32[]{:S(2)}) collective-permute-start(bf16[2,128,128]{2,1,0:T(8,128)(2,1)} %bitcast.15), channel_id=1, source_target_pairs={{0,16},{16,0},{32,48},{48,32},{64,80},{80,64},{96,112},{112,96},{1... | collective-permute-start | bytes 196616 | tf_op jit(solution)/shard_map/ppermute | solution.py:23
  4.2 8.9 %collective-permute-start = (bf16[2,128,128]{2,1,0:T(8,128)(2,1)}, bf16[2,128,128]{2,1,0:T(8,128)(2,1)S(1)}, u32[]{:S(2)}, u32[]{:S(2)}) collective-permute-start(bf16[2,128,128]{2,1,0:T(8,128)(2,1)} %bitcast.16), channel_id=1, source_target_pairs={{0,8},{1,9},{2,10},{3,11},{4,12},{5,13},{6,14},{7,15},{8,0},{9,1},... | collective-permute-start | bytes 196616 | tf_op jit(solution)/shard_map/ppermute | solution.py:19
  8.3 4.9 %copy-start.1 = (bf16[2,1,128,128]{3,2,1,0:T(8,128)(2,1)S(1)}, bf16[2,1,128,128]{3,2,1,0:T(8,128)(2,1)}, u32[]{:S(2)}) copy-start(bf16[2,1,128,128]{3,2,1,0:T(8,128)(2,1)} %param.6) | copy-start | bytes 196612
  13.2 6.3 %collective-permute-start.1 = (bf16[4,128,128]{2,1,0:T(8,128)(2,1)S(1)}, bf16[4,128,128]{2,1,0:T(8,128)(2,1)S(1)}, u32[]{:S(2)}, u32[]{:S(2)}) collective-permute-start(bf16[4,128,128]{2,1,0:T(8,128)(2,1)S(1)} %pad_maximum_fusion.2), channel_id=1, source_target_pairs={{0,4},{1,5},{2,6},{3,7},{4,0},{5,1},{6,2},{7,3},{8,12},{9,13},{10,... | collective-permute-start | bytes 393224 | tf_op jit(solution)/shard_map/ppermute | solution.py:19
  13.7 6.6 %collective-permute-start.5 = (bf16[4,128,128]{2,1,0:T(8,128)(2,1)S(1)}, bf16[4,128,128]{2,1,0:T(8,128)(2,1)S(1)}, u32[]{:S(2)}, u32[]{:S(2)}) collective-permute-start(bf16[4,128,128]{2,1,0:T(8,128)(2,1)S(1)} %pad_maximum_fusion.3), channel_id=1, source_target_pairs={{0,64},{16,80},{32,96},{48,112},{64,0},{80,16},{96,32},{112,48},{1... | collective-permute-start | bytes 393224 | tf_op jit(solution)/shard_map/ppermute | solution.py:23
  19.6 9.9 %collective-permute-start.2 = (bf16[8,128,128]{2,1,0:T(8,128)(2,1)S(1)}, bf16[8,128,128]{2,1,0:T(8,128)(2,1)S(1)}, u32[]{:S(2)}, u32[]{:S(2)}) collective-permute-start(bf16[8,128,128]{2,1,0:T(8,128)(2,1)S(1)} %pad_maximum_fusion), channel_id=1, source_target_pairs={{0,2},{1,3},{2,0},{3,1},{4,6},{5,7},{6,4},{7,5},{8,10},{9,11},{10,... | collective-permute-start | bytes 786440 | tf_op jit(solution)/shard_map/ppermute | solution.py:19
  20.4 6.4 %collective-permute-start.6 = (bf16[8,128,128]{2,1,0:T(8,128)(2,1)S(1)}, bf16[8,128,128]{2,1,0:T(8,128)(2,1)S(1)}, u32[]{:S(2)}, u32[]{:S(2)}) collective-permute-start(bf16[8,128,128]{2,1,0:T(8,128)(2,1)S(1)} %pad_maximum_fusion.1), channel_id=1, source_target_pairs={{0,32},{16,48},{32,0},{48,16},{64,96},{80,112},{96,64},{112,80},{1... | collective-permute-start | bytes 786440 | tf_op jit(solution)/shard_map/ppermute | solution.py:23
  26.9 13.3 %collective-permute-start.7 = (bf16[16,128,128]{2,1,0:T(8,128)(2,1)S(1)}, bf16[16,128,128]{2,1,0:T(8,128)(2,1)S(1)}, u32[]{:S(2)}, u32[]{:S(2)}) collective-permute-start(bf16[16,128,128]{2,1,0:T(8,128)(2,1)S(1)} %constant_dynamic-update-slice_fusion.m_ref), channel_id=1, source_target_pairs={{0,1},{1,0},{2,3},{3,2},{4,5},{5,4},{6,7},{7,6},{8,9},{9,8},{10,11... | collective-permute-start | bytes 1572872 | tf_op jit(solution)/shard_map/ppermute | solution.py:19
  40.8 11.2 %collective-permute-start.9 = (bf16[4,128,128]{2,1,0:T(8,128)(2,1)S(1)}, bf16[4,128,128]{2,1,0:T(8,128)(2,1)S(1)}, u32[]{:S(2)}, u32[]{:S(2)}) collective-permute-start(bf16[4,128,128]{2,1,0:T(8,128)(2,1)S(1)} %get-tuple-element.18), channel_id=1, source_target_pairs={{0,8},{1,9},{2,10},{3,11},{4,12},{5,13},{6,14},{7,15},{8,0},{9,1},... | collective-permute-start | bytes 393224 | tf_op jit(solution)/shard_map/ppermute | solution.py:19
  46.6 10.5 %collective-permute-start.8 = (bf16[4,128,128]{2,1,0:T(8,128)(2,1)S(1)}, bf16[4,128,128]{2,1,0:T(8,128)(2,1)S(1)}, u32[]{:S(2)}, u32[]{:S(2)}) collective-permute-start(bf16[4,128,128]{2,1,0:T(8,128)(2,1)S(1)} %shard_map.70), channel_id=1, source_target_pairs={{0,8},{1,9},{2,10},{3,11},{4,12},{5,13},{6,14},{7,15},{8,0},{9,1},... | collective-permute-start | bytes 393224 | tf_op jit(solution)/shard_map/ppermute | solution.py:19
  52.1 5.1 %collective-permute-start.10 = (bf16[4,128,128]{2,1,0:T(8,128)(2,1)S(1)}, bf16[4,128,128]{2,1,0:T(8,128)(2,1)S(1)}, u32[]{:S(2)}, u32[]{:S(2)}) collective-permute-start(bf16[4,128,128]{2,1,0:T(8,128)(2,1)S(1)} %add_convert_fusion), channel_id=1, source_target_pairs={{0,4},{1,5},{2,6},{3,7},{4,0},{5,1},{6,2},{7,3},{8,12},{9,13},{10,... | collective-permute-start | bytes 393224 | tf_op jit(solution)/shard_map/ppermute | solution.py:19
  53.2 4.8 %copy-start.3 = (f32[128]{0:T(128)S(1)}, f32[128]{0:T(128)}, u32[]{:S(2)}) copy-start(f32[128]{0:T(128)} %param.11) | copy-start | bytes 1540
  53.2 4.9 %copy-start.4 = (f32[16]{0:T(128)S(1)}, f32[16]{0:T(128)}, u32[]{:S(2)}) copy-start(f32[16]{0:T(128)} %param.10) | copy-start | bytes 196
  53.2 7.2 %copy-start.2 = (bf16[2,1,128,128]{3,2,1,0:T(8,128)(2,1)S(1)}, bf16[2,1,128,128]{3,2,1,0:T(8,128)(2,1)}, u32[]{:S(2)}) copy-start(bf16[2,1,128,128]{3,2,1,0:T(8,128)(2,1)} %param.8) | copy-start | bytes 196612
  57.2 3.2 %collective-permute-start.11 = (bf16[2,128,128]{2,1,0:T(8,128)(2,1)S(1)}, bf16[2,128,128]{2,1,0:T(8,128)(2,1)S(1)}, u32[]{:S(2)}, u32[]{:S(2)}) collective-permute-start(bf16[2,128,128]{2,1,0:T(8,128)(2,1)S(1)} %slice.19), channel_id=1, source_target_pairs={{0,2},{1,3},{2,0},{3,1},{4,6},{5,7},{6,4},{7,5},{8,10},{9,11},{10,... | collective-permute-start | bytes 196616 | tf_op jit(solution)/shard_map/ppermute | solution.py:19

commit v4 on v3

--- a/solution.py
+++ b/solution.py
@@ -150,12 +150,12 @@
         line = lax.broadcasted_iota(jnp.int32, (256, 32), 0) >> 4
         pair = lax.broadcasted_iota(jnp.int32, (256, 32), 1)
         slot, ii = line >> 1, line & 1
-        rows = jnp.where(pair == (ii << 4) + (c ^ (slot << 1)), 1.0, 0.0).astype(BF)
+        rows = jnp.where(pair == (ii << 4) + (c ^ (slot << 1) ^ (slot & 4)), 1.0, 0.0).astype(BF)
         picked = jnp.dot(rows, h_ref[...], preferred_element_type=F32).astype(BF)
         true = lax.broadcasted_iota(jnp.int32, (256, 512), 0)
         here = lax.broadcasted_iota(jnp.int32, (256, 512), 1)
         par, d, kk = here >> 8, (here >> 5) & 7, (here >> 4) & 1
-        mask = (d & 1) | ((d & 2) << 1) | ((d & 4) >> 1)
+        mask = (d & 1) ^ (d & 2) ^ ((d & 2) << 1) ^ ((d & 4) >> 1)
         wanted = ((((r ^ mask) << 1) + kk) << 4) + (c ^ par)
         cols = jnp.where(true == wanted, 1.0, 0.0).astype(BF)
         wide = jnp.dot(picked, cols, preferred_element_type=F32)
@@ -167,7 +167,7 @@
         out_specs=VMEM,
         out_shape=jax.ShapeDtypeStruct((256, 512), BF),
         compiler_params=params(8),
-        cost_estimate=cost(10**8, 10**6),
+        cost_estimate=cost(10**9, 10**6),
         name="spread",
     )(where, ints)
 
@@ -207,16 +207,18 @@
     where = jnp.stack([r, c]).astype(jnp.int32)
     own = t_amps.reshape(2, V, V)
     others = col_swap(df_slabs, 1)
-    got_y2 = col_swap(own, 8)
+    got_y2 = col_swap(own, 12)
     rows1 = row_swap(own, 1)
     ints = lax.dynamic_slice_in_dim(hole_ints, r * 2, 2, 0).reshape(32, 256)
-    first, where, ints = lax.optimization_barrier((own, where, ints))
+    where, ints = lax.optimization_barrier((where, ints))
     wide = spread_ints(ints, where)
-    part_0, slabs = ladder([(first, 0, 2)], df_slabs, [], pull=True, chunk=16)
+    first, wide = lax.optimization_barrier((own, wide))
+    slabs = df_slabs
+    part_0 = ladder([(first, 0, 2)], slabs, [], chunk=16)
     near = jnp.concatenate([own, got_y2])
     got_y1 = col_swap(near, 4)
     two_rows = jnp.concatenate([first, rows1])
-    rows2 = row_swap(two_rows, 4)
+    rows2 = row_swap(two_rows, 6)
     part_4 = ladder([(got_y2, 0, 2)], slabs, [], chunk=16)
     got_x = col_swap(jnp.concatenate([near, got_y1]), 2)
     four_rows = jnp.concatenate([two_rows, rows2])
@@ -233,9 +235,9 @@
 
     full_67 = more(got_y1, part_26, 2, 6)
     send_67, hole = hole_terms(wide, mine, other, full_67)
-    back_23 = col_swap(send_67, 8).astype(F32)
+    back_23 = col_swap(send_67, 12).astype(F32)
     send_45 = more(got_y2, part_4, 0, 2, [(hole, 8, 4)], BF)
-    back_01 = col_swap(send_45, 8).astype(F32)
+    back_01 = col_swap(send_45, 12).astype(F32)
     full_23 = more(got_y1, part_26, 0, 4, [(hole, 4, 4)])
     near_01 = col_swap((full_23 + back_23).astype(BF), 4).astype(F32)
     full_01 = more(first, part_0, 0, 0, [(hole, 0, 4)])

time: 62.7 us -> 66.3 us (1.057)
  the two profiles are of different devices: /device:TPU:1 before, /device:TPU:8 now
where the time goes in v4:
time: 66.3 us; the launch traced here: 66.1 us
  Pallas kernels  38.5 us (58%)
  starting transfers between devices  17.1 us (26%)
  waiting for transfers between devices  6.91 us (10%)
  other arithmetic  1.74 us (3%)
  local copies, waits for them, and re-layouts  1.47 us (2%)
    pallas_call x8, Pallas kernels, ladder(): pl.pallas_call(kern, in_specs=specs, out_specs=[VMEM] * len(shapes), out_...  37 us
    ppermute x9, starting transfers between devices, col_swap(): return lax.ppermute(x, 'col', [(c, c ^ mask) for c in range(16)])  9.83 us
    ppermute x3, starting transfers between devices, row_swap(): return lax.ppermute(x, 'row', [(r, r ^ mask) for r in range(8)])  7.3 us
    ppermute x9, waiting for transfers between devices, col_swap(): return lax.ppermute(x, 'col', [(c, c ^ mask) for c in range(16)])  5.02 us
    ppermute x3, waiting for transfers between devices, row_swap(): return lax.ppermute(x, 'row', [(r, r ^ mask) for r in range(8)])  1.88 us
    reshape x1, other arithmetic, body(): ((drive.reshape(2, V, V).astype(F32) + total) / denom).reshape(2, 1, V, V)  1.43 us
  transfers between devices with their start and end apart: 12, of which 5 were waited for; matrix products, arithmetic and copies ran while one was open for 2% of the time, Pallas kernels for 49%

profile of v4, /device:TPU:8, one launch (start us, length us, event | category | flops | bytes accessed | tf_op | source)
XLA Modules:
  0.0 66.1 jit_solution(15246590370686630298)
XLA Ops:
  0.0 3.1 %collective-permute-start.4 = (bf16[2,128,128]{2,1,0:T(8,128)(2,1)}, bf16[2,128,128]{2,1,0:T(8,128)(2,1)S(1)}, u32[]{:S(2)}, u32[]{:S(2)}) collective-permute-start(bf16[2,128,128]{2,1,0:T(8,128)(2,1)} %bitcast.15), channel_id=1, source_target_pairs={{0,16},{16,0},{32,48},{48,32},{64,80},{80,64},{96,112},{112,96},{1... | collective-permute-start | bytes 196616 | tf_op jit(solution)/shard_map/ppermute | solution.py:23
  3.1 1.6 %collective-permute-start = (bf16[2,128,128]{2,1,0:T(8,128)(2,1)}, bf16[2,128,128]{2,1,0:T(8,128)(2,1)S(1)}, u32[]{:S(2)}, u32[]{:S(2)}) collective-permute-start(bf16[2,128,128]{2,1,0:T(8,128)(2,1)} %bitcast.16), channel_id=1, source_target_pairs={{0,12},{1,13},{2,14},{3,15},{4,8},{5,9},{6,10},{7,11},{8,4},{9,5},... | collective-permute-start | bytes 196616 | tf_op jit(solution)/shard_map/ppermute | solution.py:19
  4.9 0.9 %spread.1.w_ref = bf16[256,512]{1,0:T(8,128)(2,1)S(1)} custom-call(s32[2]{0:T(128)S(1)} %pad_add_fusion.w_ref, bf16[32,256]{1,0:T(8,128)(2,1)S(1)} %reshape.47.h_ref), custom_call_target="tpu_custom_call" | custom-call | flops 1000000000 | bytes 1000000 | tf_op jit(solution)/shard_map/spread/pallas_call | solution.py:164
  6.3 2.1 %shard_map.64.refs_3_ = f32[2,128,128]{2,1,0:T(8,128)S(1)} custom-call(bf16[2,128,128]{2,1,0:T(8,128)(2,1)S(1)} %bitcast.18, bf16[64,128,128]{2,1,0:T(8,128)(2,1)S(1)} %copy-done.2), custom_call_target="tpu_custom_call" | custom-call | flops 1073741824 | bytes 2097152 | tf_op jit(solution)/shard_map/pallas_call | solution.py:135
  8.4 4.1 %collective-permute-start.5 = (bf16[4,128,128]{2,1,0:T(8,128)(2,1)S(1)}, bf16[4,128,128]{2,1,0:T(8,128)(2,1)S(1)}, u32[]{:S(2)}, u32[]{:S(2)}) collective-permute-start(bf16[4,128,128]{2,1,0:T(8,128)(2,1)S(1)} %pad_maximum_fusion.3), channel_id=1, source_target_pairs={{0,96},{16,112},{32,64},{48,80},{64,32},{80,48},{96,0},{112,16},{1... | collective-permute-start | bytes 393224 | tf_op jit(solution)/shard_map/ppermute | solution.py:23
  12.6 2.0 %collective-permute-start.1 = (bf16[4,128,128]{2,1,0:T(8,128)(2,1)S(1)}, bf16[4,128,128]{2,1,0:T(8,128)(2,1)S(1)}, u32[]{:S(2)}, u32[]{:S(2)}) collective-permute-start(bf16[4,128,128]{2,1,0:T(8,128)(2,1)S(1)} %pad_maximum_fusion.2), channel_id=1, source_target_pairs={{0,4},{1,5},{2,6},{3,7},{4,0},{5,1},{6,2},{7,3},{8,12},{9,13},{10,... | collective-permute-start | bytes 393224 | tf_op jit(solution)/shard_map/ppermute | solution.py:19
  14.5 2.1 %shard_map.69.refs_3_ = f32[2,128,128]{2,1,0:T(8,128)S(1)} custom-call(bf16[2,128,128]{2,1,0:T(8,128)(2,1)S(1)} %collective-permute-done.refs_0_, bf16[64,128,128]{2,1,0:T(8,128)(2,1)S(1)} %copy-done.2), custom_call_target="tpu_custom_call" | custom-call | flops 1073741824 | bytes 2097152 | tf_op jit(solution)/shard_map/pallas_call | solution.py:135
  16.8 1.0 %collective-permute-done.1.refs_0_ = bf16[4,128,128]{2,1,0:T(8,128)(2,1)S(1)} collective-permute-done((bf16[4,128,128]{2,1,0:T(8,128)(2,1)S(1)}, bf16[4,128,128]{2,1,0:T(8,128)(2,1)S(1)}, u32[]{:S(2)}, u32[]{:S(2)}) %collective-permute-start.1) | collective-permute-done | bytes 131104 | tf_op jit(solution)/shard_map/ppermute | solution.py:19
  17.8 0.7 %collective-permute-start.2 = (bf16[8,128,128]{2,1,0:T(8,128)(2,1)S(1)}, bf16[8,128,128]{2,1,0:T(8,128)(2,1)S(1)}, u32[]{:S(2)}, u32[]{:S(2)}) collective-permute-start(bf16[8,128,128]{2,1,0:T(8,128)(2,1)S(1)} %pad_maximum_fusion), channel_id=1, source_target_pairs={{0,2},{1,3},{2,0},{3,1},{4,6},{5,7},{6,4},{7,5},{8,10},{9,11},{10,... | collective-permute-start | bytes 786440 | tf_op jit(solution)/shard_map/ppermute | solution.py:19
  18.5 3.9 %shard_map.66.refs_3_ = f32[4,128,128]{2,1,0:T(8,128)S(1)} custom-call(bf16[4,128,128]{2,1,0:T(8,128)(2,1)S(1)} %collective-permute-done.1.refs_0_, bf16[64,128,128]{2,1,0:T(8,128)(2,1)S(1)} %copy-done.2), custom_call_target="tpu_custom_call" | custom-call | flops 2147483648 | bytes 2097152 | tf_op jit(solution)/shard_map/pallas_call | solution.py:135
  22.4 1.9 %collective-permute-done.6 = bf16[8,128,128]{2,1,0:T(8,128)(2,1)S(1)} collective-permute-done((bf16[8,128,128]{2,1,0:T(8,128)(2,1)S(1)}, bf16[8,128,128]{2,1,0:T(8,128)(2,1)S(1)}, u32[]{:S(2)}, u32[]{:S(2)}) %collective-permute-start.6) | collective-permute-done | bytes 262176 | tf_op jit(solution)/shard_map/ppermute | solution.py:23
  25.0 6.7 %shard_map.65.refs_4_ = f32[8,128,128]{2,1,0:T(8,128)S(1)} custom-call(bf16[8,128,128]{2,1,0:T(8,128)(2,1)S(1)} %collective-permute-done.2.refs_0_.refs_1_, bf16[64,128,128]{2,1,0:T(8,128)(2,1)S(1)} %copy-done.2), custom_call_target="tpu_custom_call" | custom-call | flops 4294967296 | bytes 2097152 | tf_op jit(solution)/shard_map/pallas_call | solution.py:135
  31.7 5.5 %shard_map.67.a_ref = f32[4,128,128]{2,1,0:T(8,128)S(1)} custom-call(bf16[4,128,128]{2,1,0:T(8,128)(2,1)S(1)} %collective-permute-done.1.refs_0_, bf16[8,128,128]{2,1,0:T(8,128)(2,1)S(1)} %collective-permute-done.2.refs_0_.refs_1_, bf16[64,128,128]{2,1,0:T(8,128)(2,1)} %collective-permute-done.3.refs_2_, f32[4,128,128]{2,1,0:T(8,128)S(1)} %shard_map.66.refs_3_, ...), custom_call_target="tpu_custom_call" | custom-call | flops 2147483648 | bytes 2097152 | tf_op jit(solution)/shard_map/pallas_call | solution.py:135
  37.2 0.7 %hole.1 = (bf16[4,128,128]{2,1,0:T(8,128)(2,1)S(1)}, f32[12,128,128]{2,1,0:T(8,128)S(1)}) custom-call(bf16[256,512]{1,0:T(8,128)(2,1)S(1)} %spread.1.w_ref, bf16[16,128,128]{2,1,0:T(8,128)(2,1)S(1)} %constant_dynamic-update-slice_fusion.m_ref, bf16[16,128,128]{2,1,0:T(8,128)(2,1)S(1)} %collective-permute-done.7.p_ref, f32[4,128,128]{2,1,0:T(8,128)S(1)} %shard_map.67.a_ref), custom_call_target="tpu_custom_call" | custom-call | flops 1000000000 | bytes 1000000 | tf_op jit(solution)/shard_map/hole/pallas_call | solution.py:190
  37.9 5.7 %shard_map.70 = bf16[4,128,128]{2,1,0:T(8,128)(2,1)S(1)} custom-call(bf16[2,128,128]{2,1,0:T(8,128)(2,1)S(1)} %collective-permute-done.refs_0_, bf16[8,128,128]{2,1,0:T(8,128)(2,1)S(1)} %collective-permute-done.2.refs_0_.refs_1_, bf16[64,128,128]{2,1,0:T(8,128)(2,1)} %collective-permute-done.3.refs_2_, f32[2,128,128]{2,1,0:T(8,128)S(1)} %shard_map.69.refs_3_, ...), custom_call_target="tpu_custom_call" | custom-call | flops 2147483648 | bytes 2097152 | tf_op jit(solution)/shard_map/pallas_call | solution.py:135
  43.9 1.9 %collective-permute-start.9 = (bf16[4,128,128]{2,1,0:T(8,128)(2,1)S(1)}, bf16[4,128,128]{2,1,0:T(8,128)(2,1)S(1)}, u32[]{:S(2)}, u32[]{:S(2)}) collective-permute-start(bf16[4,128,128]{2,1,0:T(8,128)(2,1)S(1)} %get-tuple-element.16), channel_id=1, source_target_pairs={{0,12},{1,13},{2,14},{3,15},{4,8},{5,9},{6,10},{7,11},{8,4},{9,5},... | collective-permute-start | bytes 393224 | tf_op jit(solution)/shard_map/ppermute | solution.py:19
  45.7 5.5 %shard_map.71 = f32[4,128,128]{2,1,0:T(8,128)S(1)} custom-call(bf16[4,128,128]{2,1,0:T(8,128)(2,1)S(1)} %collective-permute-done.1.refs_0_, bf16[8,128,128]{2,1,0:T(8,128)(2,1)S(1)} %collective-permute-done.2.refs_0_.refs_1_, bf16[64,128,128]{2,1,0:T(8,128)(2,1)} %collective-permute-done.3.refs_2_, f32[4,128,128]{2,1,0:T(8,128)S(1)} %shard_map.66.refs_3_, ...), custom_call_target="tpu_custom_call" | custom-call | flops 2147483648 | bytes 2097152 | tf_op jit(solution)/shard_map/pallas_call | solution.py:135
  51.2 0.8 %collective-permute-done.9 = bf16[4,128,128]{2,1,0:T(8,128)(2,1)S(1)} collective-permute-done((bf16[4,128,128]{2,1,0:T(8,128)(2,1)S(1)}, bf16[4,128,128]{2,1,0:T(8,128)(2,1)S(1)}, u32[]{:S(2)}, u32[]{:S(2)}) %collective-permute-start.9) | collective-permute-done | bytes 131104 | tf_op jit(solution)/shard_map/ppermute | solution.py:19
  52.1 2.6 %collective-permute-start.10 = (bf16[4,128,128]{2,1,0:T(8,128)(2,1)S(1)}, bf16[4,128,128]{2,1,0:T(8,128)(2,1)S(1)}, u32[]{:S(2)}, u32[]{:S(2)}) collective-permute-start(bf16[4,128,128]{2,1,0:T(8,128)(2,1)S(1)} %add_convert_fusion), channel_id=1, source_target_pairs={{0,4},{1,5},{2,6},{3,7},{4,0},{5,1},{6,2},{7,3},{8,12},{9,13},{10,... | collective-permute-start | bytes 393224 | tf_op jit(solution)/shard_map/ppermute | solution.py:19
  54.7 5.5 %shard_map.68 = f32[4,128,128]{2,1,0:T(8,128)S(1)} custom-call(bf16[2,128,128]{2,1,0:T(8,128)(2,1)S(1)} %bitcast.23, bf16[8,128,128]{2,1,0:T(8,128)(2,1)S(1)} %collective-permute-done.2.refs_0_.refs_1_, bf16[64,128,128]{2,1,0:T(8,128)(2,1)} %collective-permute-done.3.refs_2_, f32[2,128,128]{2,1,0:T(8,128)S(1)} %shard_map.64.refs_3_, ...), custom_call_target="tpu_custom_call" | custom-call | flops 2147483648 | bytes 2097152 | tf_op jit(solution)/shard_map/pallas_call | solution.py:135
  60.3 0.7 %collective-permute-start.11 = (bf16[2,128,128]{2,1,0:T(8,128)(2,1)S(1)}, bf16[2,128,128]{2,1,0:T(8,128)(2,1)S(1)}, u32[]{:S(2)}, u32[]{:S(2)}) collective-permute-start(bf16[2,128,128]{2,1,0:T(8,128)(2,1)S(1)} %slice.19), channel_id=1, source_target_pairs={{0,2},{1,3},{2,0},{3,1},{4,6},{5,7},{6,4},{7,5},{8,10},{9,11},{10,... | collective-permute-start | bytes 196616 | tf_op jit(solution)/shard_map/ppermute | solution.py:19
  61.1 0.7 dynamic_slice.11
  61.8 2.8 %collective-permute-done.11 = bf16[2,128,128]{2,1,0:T(8,128)(2,1)S(1)} collective-permute-done((bf16[2,128,128]{2,1,0:T(8,128)(2,1)S(1)}, bf16[2,128,128]{2,1,0:T(8,128)(2,1)S(1)}, u32[]{:S(2)}, u32[]{:S(2)}) %collective-permute-start.11) | collective-permute-done | bytes 65568 | tf_op jit(solution)/shard_map/ppermute | solution.py:19
  64.6 1.4 %fusion.2 = f32[2,1,128,128]{3,2,1,0:T(8,128)} fusion(f32[4,128,128]{2,1,0:T(8,128)S(1)} %convert_add_fusion, bf16[2,128,128]{2,1,0:T(8,128)(2,1)S(1)} %collective-permute-done.11, bf16[2,1,128,128]{3,2,1,0:T(8,128)(2,1)S(1)} %copy-done.3, f32[]{:T(128)} %bitcast.5, f32[2]{0:T(128)S(1)} %dynamic_slice.10, f32[128,128]{1,0:T(8,128)S(1)} %broadcast_add_fusion), kind=kLoop, calls=%fused_computation.8 | loop fusion | flops 229376 | bytes 458764 | tf_op jit(solution)/shard_map/reshape | solution.py:255
  (40 shorter events, 2.1 us)
Async XLA Ops:
  0.0 4.7 %copy-start = (bf16[16,16,16,16]{3,2,1,0:T(8,128)(2,1)S(1)}, bf16[16,16,16,16]{3,2,1,0:T(8,128)(2,1)}, u32[]{:S(2)}) copy-start(bf16[16,16,16,16]{3,2,1,0:T(8,128)(2,1)} %param.9) | copy-start | bytes 393220
  0.0 5.8 %copy-start.1 = (bf16[2,1,128,128]{3,2,1,0:T(8,128)(2,1)S(1)}, bf16[2,1,128,128]{3,2,1,0:T(8,128)(2,1)}, u32[]{:S(2)}) copy-start(bf16[2,1,128,128]{3,2,1,0:T(8,128)(2,1)} %param.6) | copy-start | bytes 196612
  0.0 31.7 %collective-permute-start.3 = (bf16[64,128,128]{2,1,0:T(8,128)(2,1)}, bf16[64,128,128]{2,1,0:T(8,128)(2,1)}, u32[]{:S(2)}, u32[]{:S(2)}) collective-permute-start(bf16[64,128,128]{2,1,0:T(8,128)(2,1)} %refs_1_.7), channel_id=1, source_target_pairs={{0,1},{1,0},{2,3},{3,2},{4,5},{5,4},{6,7},{7,6},{8,9},{9,8},{10,11... | collective-permute-start | bytes 6291464 | tf_op jit(solution)/shard_map/ppermute | solution.py:19
  0.0 8.4 %collective-permute-start.4 = (bf16[2,128,128]{2,1,0:T(8,128)(2,1)}, bf16[2,128,128]{2,1,0:T(8,128)(2,1)S(1)}, u32[]{:S(2)}, u32[]{:S(2)}) collective-permute-start(bf16[2,128,128]{2,1,0:T(8,128)(2,1)} %bitcast.15), channel_id=1, source_target_pairs={{0,16},{16,0},{32,48},{48,32},{64,80},{80,64},{96,112},{112,96},{1... | collective-permute-start | bytes 196616 | tf_op jit(solution)/shard_map/ppermute | solution.py:23
  3.1 9.4 %collective-permute-start = (bf16[2,128,128]{2,1,0:T(8,128)(2,1)}, bf16[2,128,128]{2,1,0:T(8,128)(2,1)S(1)}, u32[]{:S(2)}, u32[]{:S(2)}) collective-permute-start(bf16[2,128,128]{2,1,0:T(8,128)(2,1)} %bitcast.16), channel_id=1, source_target_pairs={{0,12},{1,13},{2,14},{3,15},{4,8},{5,9},{6,10},{7,11},{8,4},{9,5},... | collective-permute-start | bytes 196616 | tf_op jit(solution)/shard_map/ppermute | solution.py:19
  4.7 1.6 %copy-start.2 = (bf16[64,128,128]{2,1,0:T(8,128)(2,1)S(1)}, bf16[64,128,128]{2,1,0:T(8,128)(2,1)}, u32[]{:S(2)}) copy-start(bf16[64,128,128]{2,1,0:T(8,128)(2,1)} %refs_1_.7) | copy-start | bytes 6291460
  8.4 8.2 %collective-permute-start.5 = (bf16[4,128,128]{2,1,0:T(8,128)(2,1)S(1)}, bf16[4,128,128]{2,1,0:T(8,128)(2,1)S(1)}, u32[]{:S(2)}, u32[]{:S(2)}) collective-permute-start(bf16[4,128,128]{2,1,0:T(8,128)(2,1)S(1)} %pad_maximum_fusion.3), channel_id=1, source_target_pairs={{0,96},{16,112},{32,64},{48,80},{64,32},{80,48},{96,0},{112,16},{1... | collective-permute-start | bytes 393224 | tf_op jit(solution)/shard_map/ppermute | solution.py:23
  12.6 5.2 %collective-permute-start.1 = (bf16[4,128,128]{2,1,0:T(8,128)(2,1)S(1)}, bf16[4,128,128]{2,1,0:T(8,128)(2,1)S(1)}, u32[]{:S(2)}, u32[]{:S(2)}) collective-permute-start(bf16[4,128,128]{2,1,0:T(8,128)(2,1)S(1)} %pad_maximum_fusion.2), channel_id=1, source_target_pairs={{0,4},{1,5},{2,6},{3,7},{4,0},{5,1},{6,2},{7,3},{8,12},{9,13},{10,... | collective-permute-start | bytes 393224 | tf_op jit(solution)/shard_map/ppermute | solution.py:19
  16.7 7.6 %collective-permute-start.6 = (bf16[8,128,128]{2,1,0:T(8,128)(2,1)S(1)}, bf16[8,128,128]{2,1,0:T(8,128)(2,1)S(1)}, u32[]{:S(2)}, u32[]{:S(2)}) collective-permute-start(bf16[8,128,128]{2,1,0:T(8,128)(2,1)S(1)} %pad_maximum_fusion.1), channel_id=1, source_target_pairs={{0,32},{16,48},{32,0},{48,16},{64,96},{80,112},{96,64},{112,80},{1... | collective-permute-start | bytes 786440 | tf_op jit(solution)/shard_map/ppermute | solution.py:23
  17.8 7.2 %collective-permute-start.2 = (bf16[8,128,128]{2,1,0:T(8,128)(2,1)S(1)}, bf16[8,128,128]{2,1,0:T(8,128)(2,1)S(1)}, u32[]{:S(2)}, u32[]{:S(2)}) collective-permute-start(bf16[8,128,128]{2,1,0:T(8,128)(2,1)S(1)} %pad_maximum_fusion), channel_id=1, source_target_pairs={{0,2},{1,3},{2,0},{3,1},{4,6},{5,7},{6,4},{7,5},{8,10},{9,11},{10,... | collective-permute-start | bytes 786440 | tf_op jit(solution)/shard_map/ppermute | solution.py:19
  24.3 12.9 %collective-permute-start.7 = (bf16[16,128,128]{2,1,0:T(8,128)(2,1)S(1)}, bf16[16,128,128]{2,1,0:T(8,128)(2,1)S(1)}, u32[]{:S(2)}, u32[]{:S(2)}) collective-permute-start(bf16[16,128,128]{2,1,0:T(8,128)(2,1)S(1)} %constant_dynamic-update-slice_fusion.m_ref), channel_id=1, source_target_pairs={{0,1},{1,0},{2,3},{3,2},{4,5},{5,4},{6,7},{7,6},{8,9},{9,8},{10,11... | collective-permute-start | bytes 1572872 | tf_op jit(solution)/shard_map/ppermute | solution.py:19
  43.6 16.6 %collective-permute-start.8 = (bf16[4,128,128]{2,1,0:T(8,128)(2,1)S(1)}, bf16[4,128,128]{2,1,0:T(8,128)(2,1)S(1)}, u32[]{:S(2)}, u32[]{:S(2)}) collective-permute-start(bf16[4,128,128]{2,1,0:T(8,128)(2,1)S(1)} %shard_map.70), channel_id=1, source_target_pairs={{0,12},{1,13},{2,14},{3,15},{4,8},{5,9},{6,10},{7,11},{8,4},{9,5},... | collective-permute-start | bytes 393224 | tf_op jit(solution)/shard_map/ppermute | solution.py:19
  43.9 8.2 %collective-permute-start.9 = (bf16[4,128,128]{2,1,0:T(8,128)(2,1)S(1)}, bf16[4,128,128]{2,1,0:T(8,128)(2,1)S(1)}, u32[]{:S(2)}, u32[]{:S(2)}) collective-permute-start(bf16[4,128,128]{2,1,0:T(8,128)(2,1)S(1)} %get-tuple-element.16), channel_id=1, source_target_pairs={{0,12},{1,13},{2,14},{3,15},{4,8},{5,9},{6,10},{7,11},{8,4},{9,5},... | collective-permute-start | bytes 393224 | tf_op jit(solution)/shard_map/ppermute | solution.py:19
  52.1 8.9 %copy-start.4 = (f32[128]{0:T(128)S(1)}, f32[128]{0:T(128)}, u32[]{:S(2)}) copy-start(f32[128]{0:T(128)} %param.11) | copy-start | bytes 1540
  52.1 8.9 %copy-start.5 = (f32[16]{0:T(128)S(1)}, f32[16]{0:T(128)}, u32[]{:S(2)}) copy-start(f32[16]{0:T(128)} %param.10) | copy-start | bytes 196
  52.1 12.5 %copy-start.3 = (bf16[2,1,128,128]{3,2,1,0:T(8,128)(2,1)S(1)}, bf16[2,1,128,128]{3,2,1,0:T(8,128)(2,1)}, u32[]{:S(2)}) copy-start(bf16[2,1,128,128]{3,2,1,0:T(8,128)(2,1)} %param.8) | copy-start | bytes 196612
  52.1 8.1 %collective-permute-start.10 = (bf16[4,128,128]{2,1,0:T(8,128)(2,1)S(1)}, bf16[4,128,128]{2,1,0:T(8,128)(2,1)S(1)}, u32[]{:S(2)}, u32[]{:S(2)}) collective-permute-start(bf16[4,128,128]{2,1,0:T(8,128)(2,1)S(1)} %add_convert_fusion), channel_id=1, source_target_pairs={{0,4},{1,5},{2,6},{3,7},{4,0},{5,1},{6,2},{7,3},{8,12},{9,13},{10,... | collective-permute-start | bytes 393224 | tf_op jit(solution)/shard_map/ppermute | solution.py:19
  60.3 4.3 %collective-permute-start.11 = (bf16[2,128,128]{2,1,0:T(8,128)(2,1)S(1)}, bf16[2,128,128]{2,1,0:T(8,128)(2,1)S(1)}, u32[]{:S(2)}, u32[]{:S(2)}) collective-permute-start(bf16[2,128,128]{2,1,0:T(8,128)(2,1)S(1)} %slice.19), channel_id=1, source_target_pairs={{0,2},{1,3},{2,0},{3,1},{4,6},{5,7},{6,4},{7,5},{8,10},{9,11},{10,... | collective-permute-start | bytes 196616 | tf_op jit(solution)/shard_map/ppermute | solution.py:19
